TPU v7x, 256 devices: a whole 4x4x8 slice. The times are simulated.
256 devices in a mesh: section: 2 (over core), dp: 16 (over z, x_lo), tensor: 8 (over y, x_hi).
Axes of the slice: x: 4 (x_hi: 2, x_lo: 2; x = x_hi * 2 + x_lo), y: 4, z: 8, core: 2. Of those that a mesh axis runs over, the one named last changes fastest.
Arguments:
- tokens: bfloat16 [2048, 4096], P('dp', 'tensor'), may hold values from -6 to 6
- gain: bfloat16 [2, 4096], P('section', 'tensor'), may hold values from 0.099609375 to 1.8984375
- w_up: bfloat16 [2, 4096, 5120], P('section', 'dp', 'tensor'), may hold values from -0.09375 to 0.09375
- w_down: bfloat16 [2, 5120, 4096], P('section', 'tensor', 'dp'), may hold values from -0.078125 to 0.078125
- cotangent: bfloat16 [2, 2048, 4096], P('section', 'dp'), may hold values from -6 to 6
Outputs:
- states: bfloat16 [2, 2048, 4096], P('section', 'dp', 'tensor')
- grad_down: bfloat16 [2, 5120, 4096], P('section', 'tensor', 'dp')
All inputs are finite; a program needn't handle non-finite values.
Results may differ from a plain program's by a relative error of at most 0.02.
Values may be sent and summed in bfloat16 or wider, within the bound.
A program may use at most 64 MiB of HBM per device.

v0:
```python
import functools

import jax
import jax.numpy as jnp
from jax import lax
from jax.experimental import pallas as pl
from jax.experimental.pallas import tpu as pltpu
from jax.sharding import PartitionSpec as P

EPS = 1e-06
F32 = jnp.float32
BF16 = jnp.bfloat16


MESH = pl.DeviceIdType.MESH
ROW_CHUNK = 16


def far_first(count):
    return sorted(range(1, count), key=lambda k: abs(2 * k - count)) + [0]


def remote(src, dst, send_sem, recv_sem, target):
    return pltpu.make_async_remote_copy(
        src_ref=src,
        dst_ref=dst,
        send_sem=send_sem,
        recv_sem=recv_sem,
        device_id=target,
        device_id_type=MESH,
    )


def layer_kernel(
    sizes,
    inner,
    width,
    layer,
    is_last,
    x_ref,
    gain_ref,
    up_ref,
    down_ref,
    hid_out,
    x_out,
    state_out,
    scaled,
    sum_send,
    sum_recv,
    x_send,
    x_recv,
    z_send,
    z_recv,
    total,
    hid,
    part_send,
    part_recv,
    x_next,
    state_buf,
    sum_ss,
    sum_rs,
    x_ss,
    x_rs,
    z_ss,
    z_rs,
    up_ss,
    up_rs,
    dn_ss,
    dn_rs,
    fx_ss,
    fx_rs,
    out_sem,
    part_ss,
    part_rs,
    xn_ss,
    xn_rs,
    st_ss,
    st_rs,
    end_sem,
):
    sections, dp_count, tensors = sizes
    outer = dp_count // inner
    group = sections * tensors
    owned = dp_count // group
    per_tensor = dp_count // tensors
    core = lax.axis_index("section")
    tensor = lax.axis_index("tensor")
    member = tensor * sections + core
    me = lax.axis_index("dp")
    z = me // inner
    x = lax.rem(me, inner)
    peer = 1 - x
    rows = x_ref.shape[1]

    barrier = pltpu.get_barrier_semaphore()
    for m in range(1, dp_count):
        pl.semaphore_signal(
            barrier, inc=1, device_id={"dp": lax.rem(me + m, dp_count)}, device_id_type=MESH
        )

    def place(index):
        return {"section": lax.rem(index, sections), "tensor": index // sections}

    for off in range(1, group):
        pl.semaphore_signal(
            barrier, inc=1, device_id=place(lax.rem(member + off, group)), device_id_type=MESH
        )
    giver = lax.rem(me, group)
    for q in range(per_tensor):
        source = tensor * per_tensor + q
        apart = (giver != member) | (source != me)

        @pl.when((core == layer) & apart)
        def _():
            pl.semaphore_signal(
                barrier, inc=1, device_id={"dp": source, **place(giver)}, device_id_type=MESH
            )

    def state_is_local(block):
        return (core == layer) & (block == me) & (tensor == me // per_tensor)

    arrivals = dp_count - 1 + group - 1 + owned
    for i in range(owned):
        arrivals = arrivals - state_is_local(member + i * group).astype(jnp.int32)
    pl.semaphore_wait(barrier, arrivals)

    row_id = lax.broadcasted_iota(jnp.int32, (rows, rows), 0)
    col_id = lax.broadcasted_iota(jnp.int32, (rows, rows), 1)
    eye = row_id == col_id
    gain_f = gain_ref[...].astype(F32)

    def prepare(block, _):
        values = x_ref[block].astype(F32)
        scaled[block] = (values * gain_f).astype(BF16)
        column = jnp.sum(values * values, axis=1, keepdims=True)
        sum_send[block] = jnp.sum(jnp.where(eye, column, 0.0), axis=0, keepdims=True)
        return 0

    lax.fori_loop(0, dp_count, prepare, 0)

    order = far_first(outer)
    x_copies = {}
    for k in order:
        zz = lax.rem(z + k, outer)
        x_send[k] = jnp.dot(
            scaled[zz * inner + peer], up_ref[...], preferred_element_type=F32
        ).astype(BF16)
        x_copies[k] = remote(
            x_send.at[k], x_recv.at[k], x_ss.at[k], x_rs.at[k], {"dp": z * inner + peer}
        )
        x_copies[k].start()
    sum_copies = []
    for m in range(1, dp_count):
        target = lax.rem(me + m, dp_count)
        copy = remote(
            sum_send.at[target], sum_recv.at[m], sum_ss.at[m], sum_rs.at[m], {"dp": target}
        )
        copy.start()
        sum_copies.append(copy)
    z_copies = {}
    for k in order:
        zz = lax.rem(z + k, outer)
        mine = jnp.dot(scaled[zz * inner + x], up_ref[...], preferred_element_type=F32)
        x_copies[k].wait_recv()
        if k == 0:
            total[...] = mine + x_recv[k].astype(F32)
        else:
            z_send[k] = (mine + x_recv[k].astype(F32)).astype(BF16)
            z_copies[k] = remote(
                z_send.at[k], z_recv.at[k], z_ss.at[k], z_rs.at[k], {"dp": zz * inner + x}
            )
            z_copies[k].start()
    sums = sum_send[me]
    for m in range(1, dp_count):
        sum_copies[m - 1].wait_recv()
        sums = sums + sum_recv[m]
    inverse = lax.rsqrt(jnp.sum(jnp.where(eye, sums, 0.0), axis=1, keepdims=True) / width + EPS)
    for k in order[:-1]:
        z_copies[k].wait_recv()

    for lower in range(0, rows, ROW_CHUNK):
        rows_now = pl.ds(lower, ROW_CHUNK)
        value = total[rows_now]
        for k in order[:-1]:
            value = value + z_recv[k, rows_now].astype(F32)
        value = value * inverse[lower : lower + ROW_CHUNK]
        hid[me, rows_now] = jax.nn.gelu(value, approximate=True).astype(BF16)

    def forward(origin, sem_id):
        return remote(
            hid.at[origin * inner + x],
            hid.at[origin * inner + x],
            fx_ss.at[sem_id],
            fx_rs.at[sem_id],
            {"dp": z * inner + peer},
        )

    def expect(origin, sem_id):
        return remote(
            hid.at[origin * inner + peer],
            hid.at[origin * inner + peer],
            fx_ss.at[sem_id],
            fx_rs.at[sem_id],
            {"dp": z * inner + peer},
        )

    def hop(origin, target, sends, recvs, j):
        return remote(
            hid.at[origin * inner + x],
            hid.at[origin * inner + x],
            sends.at[j],
            recvs.at[j],
            {"dp": target * inner + x},
        )

    def landing(origin, sends, recvs, j):
        return remote(
            hid.at[origin * inner + x],
            hid.at[origin * inner + x],
            sends.at[j],
            recvs.at[j],
            {"dp": z * inner + peer},
        )

    def store(block):
        return pltpu.make_async_copy(hid.at[block], hid_out.at[block], out_sem.at[block])

    def part_copy(block):
        return remote(
            part_send.at[block],
            part_recv.at[block // group, member],
            part_ss.at[block],
            part_rs.at[(block // group) * group + member],
            place(lax.rem(block, group)),
        )

    def part_landing(block, off):
        source = lax.rem(member + off, group)
        return remote(
            part_send.at[block],
            part_recv.at[block // group, source],
            part_ss.at[block],
            part_rs.at[(block // group) * group + source],
            place(source),
        )

    def next_copy(block, off):
        return remote(
            x_next.at[block],
            x_next.at[block],
            xn_ss.at[(block // group) * group + off],
            xn_rs.at[block],
            place(lax.rem(member + off, group)),
        )

    slot = lax.rem(me, per_tensor)

    def state_copy(block):
        return remote(
            x_next.at[block],
            state_buf.at[slot],
            st_ss.at[block // group],
            st_rs.at[slot],
            {"section": layer, "dp": block, "tensor": me // per_tensor},
        )

    def state_local(block):
        return pltpu.make_async_copy(x_next.at[block], state_buf.at[slot], st_rs.at[slot])

    def finish(block):
        @pl.when(lax.rem(block, group) == member)
        def _():
            sum_now = part_send[block].astype(F32)
            for off in range(1, group):
                part_landing(block, off).wait_recv()
                sum_now = sum_now + part_recv[
                    block // group, lax.rem(member + off, group)
                ].astype(F32)
            x_next[block] = (x_ref[block].astype(F32) + sum_now).astype(BF16)
            if not is_last:
                for off in range(1, group):
                    next_copy(block, off).start()
            local = state_is_local(block)

            @pl.when(local)
            def _():
                state_local(block).start()

            @pl.when(jnp.logical_not(local))
            def _():
                state_copy(block).start()

    waiting = []

    def finish_oldest():
        valid, block = waiting.pop(0)
        if valid is None:
            finish(block)
        else:
            pl.when(valid)(lambda: finish(block))

    def use(block):
        store(block).start()
        part_send[block] = jnp.dot(
            hid[block], down_ref[...], preferred_element_type=F32
        ).astype(BF16)

        @pl.when(lax.rem(block, group) != member)
        def _():
            part_copy(block).start()

    def queue(valid, block):
        waiting.append((valid, block))
        if len(waiting) > 3:
            finish_oldest()

    last = outer - 1

    def start_hops(j):
        @pl.when((z - j >= 0) & (z < last))
        def _():
            hop(z - j, z + 1, up_ss, up_rs, j).start()

        @pl.when((z + j <= last) & (z > 0))
        def _():
            hop(z + j, z - 1, dn_ss, dn_rs, j).start()

    def use_peers(j):
        if j == 0:
            expect(z, 0).wait_recv()
            use(z * inner + peer)
            queue(None, z * inner + peer)
            return
        for valid, origin, sem_id in (
            (z - j >= 0, z - j, j),
            (z + j <= last, z + j, last + j),
        ):

            @pl.when(valid)
            def _():
                expect(origin, sem_id).wait_recv()
                use(origin * inner + peer)

            queue(valid, origin * inner + peer)

    start_hops(0)
    forward(z, 0).start()
    use(me)
    queue(None, me)
    for j in range(1, outer):
        above, below = z - j >= 0, z + j <= last

        @pl.when(above)
        def _():
            landing(z - j, up_ss, up_rs, j - 1).wait_recv()
            forward(z - j, j).start()

        @pl.when(below)
        def _():
            landing(z + j, dn_ss, dn_rs, j - 1).wait_recv()
            forward(z + j, last + j).start()

        if j < last:
            start_hops(j)
        for valid, origin in ((above, z - j), (below, z + j)):
            pl.when(valid)(lambda: use(origin * inner + x))
            queue(valid, origin * inner + x)
        use_peers(j - 1)
    use_peers(last)
    while waiting:
        finish_oldest()

    if not is_last:
        for block in range(dp_count):

            @pl.when(block % group != member)
            def _():
                next_copy(block, 0).wait_recv()

        pltpu.make_async_copy(x_next, x_out, end_sem.at[0]).start()

    @pl.when(core == layer)
    def _():
        stores = []
        for q in range(per_tensor):
            pltpu.make_async_copy(x_next.at[0], state_buf.at[q], st_rs.at[q]).wait()
            copy = pltpu.make_async_copy(
                state_buf.at[q],
                state_out.at[:, pl.ds(q * x_ref.shape[2], x_ref.shape[2])],
                end_sem.at[1 + q],
            )
            copy.start()
            stores.append(copy)
        for copy in stores:
            copy.wait()

    if not is_last:
        pltpu.make_async_copy(x_next, x_out, end_sem.at[0]).wait()
    for block in range(dp_count):

        @pl.when(block % group != member)
        def _():
            part_copy(block).wait_send()

    for i in range(owned):
        block = member + i * group
        if not is_last:
            for off in range(1, group):
                next_copy(block, off).wait_send()

        @pl.when(jnp.logical_not(state_is_local(block)))
        def _():
            state_copy(block).wait_send()

    for copy in list(x_copies.values()) + list(z_copies.values()) + sum_copies:
        copy.wait_send()
    forward(z, 0).wait_send()
    for j in range(last):

        @pl.when((z - j >= 0) & (z < last))
        def _():
            hop(z - j, z + 1, up_ss, up_rs, j).wait_send()

        @pl.when((z + j <= last) & (z > 0))
        def _():
            hop(z + j, z - 1, dn_ss, dn_rs, j).wait_send()

        @pl.when(z - 1 - j >= 0)
        def _():
            forward(z - 1 - j, 1 + j).wait_send()

        @pl.when(z + 1 + j <= last)
        def _():
            forward(z + 1 + j, outer + j).wait_send()

    for block in range(dp_count):
        store(block).wait()


def layer_step(layer, sizes, width, x, gain_row, up, down):
    sections, dp_count, tensors = sizes
    rows, slice_width = x.shape[1:]
    half = up.shape[1]
    inner = 2
    group = sections * tensors
    assert dp_count % inner == 0 and dp_count % group == 0
    outer = dp_count // inner
    per_tensor = dp_count // tensors
    is_last = layer == sections - 1
    dma = pltpu.SemaphoreType.DMA
    vmem = pl.BlockSpec(memory_space=pltpu.VMEM)
    hbm = pl.BlockSpec(memory_space=pl.ANY)
    wide = pltpu.VMEM((outer, rows, half), BF16)
    thin = pltpu.VMEM((dp_count, rows, slice_width), BF16)
    x_shape = x.shape if not is_last else (1, 8, 128)
    return pl.pallas_call(
        functools.partial(layer_kernel, sizes, inner, width, layer, is_last),
        name=f"layer{layer}",
        out_shape=(
            jax.ShapeDtypeStruct((dp_count, rows, half), BF16),
            jax.ShapeDtypeStruct(x_shape, BF16),
            jax.ShapeDtypeStruct((rows, per_tensor * slice_width), BF16),
        ),
        in_specs=[vmem] * 4,
        out_specs=(hbm, hbm, hbm),
        scratch_shapes=[
            thin,
            pltpu.VMEM((dp_count, 1, rows), F32),
            pltpu.VMEM((dp_count, 1, rows), F32),
            wide,
            wide,
            wide,
            wide,
            pltpu.VMEM((rows, half), F32),
            pltpu.VMEM((dp_count, rows, half), BF16),
            thin,
            pltpu.VMEM((dp_count // group, group, rows, slice_width), BF16),
            thin,
            pltpu.VMEM((per_tensor, rows, slice_width), BF16),
        ]
        + [dma((dp_count,))] * 2
        + [dma((outer,))] * 8
        + [dma((2 * outer,))] * 2
        + [dma((dp_count,))]
        + [dma((dp_count,))] * 4
        + [dma((dp_count // group,)), dma((per_tensor,)), dma((1 + per_tensor,))],
        compiler_params=pltpu.CompilerParams(collective_id=layer, has_side_effects=True),
    )(x, gain_row, up, down)


def front_kernel(
    sizes,
    tok_ref,
    gain_ref,
    up_ref,
    down_ref,
    cot_ref,
    x_out,
    gain_out0,
    gain_out1,
    up_out0,
    up_out1,
    down_out0,
    down_out1,
    cot_out,
    x_buf,
    gain_buf,
    up_buf,
    down_buf,
    cot_buf,
    tok_ss,
    tok_rs,
    ty_ss,
    tf_ss,
    tf_rs,
    cot_ss,
    cot_rs,
    cy_ss,
    cy_rs,
    gain_ss,
    gain_rs,
    w_ss,
    w_rs,
    own_sem,
    end_sem,
):
    sections, dp_count, tensors = sizes
    group = sections * tensors
    per_tensor = dp_count // tensors
    core = lax.axis_index("section")
    tensor = lax.axis_index("tensor")
    me = lax.axis_index("dp")
    other = 1 - core
    member = tensor * sections + core
    rows, slice_width = x_buf.shape[1:]
    half = up_buf.shape[2]
    half_rows = rows // sections
    part_rows = rows // tensors

    def place(index):
        return {"section": lax.rem(index, sections), "tensor": index // sections}

    barrier = pltpu.get_barrier_semaphore()

    def greet(target):
        pl.semaphore_signal(barrier, inc=1, device_id=target, device_id_type=MESH)

    for m in range(1, dp_count):
        greet({"dp": lax.rem(me + m, dp_count)})
    for off in range(1, group):
        greet(place(lax.rem(member + off, group)))
    feature_home = me // per_tensor
    at_home = feature_home == tensor
    pl.semaphore_wait(barrier, dp_count - 1 + group - 1)

    my_half = pl.ds(pl.multiple_of(core * half_rows, half_rows), half_rows)
    my_part = pl.ds(pl.multiple_of(tensor * part_rows, part_rows), part_rows)

    def columns(index, size):
        return pl.ds(pl.multiple_of(index * size, size), size)

    def token_copy(q):
        return remote(
            tok_ref.at[my_half, pl.ds(q * slice_width, slice_width)],
            x_buf.at[me, my_half],
            tok_ss.at[q],
            tok_rs.at[me],
            {"dp": tensor * per_tensor + q},
        )

    def token_local(q):
        return pltpu.make_async_copy(
            tok_ref.at[my_half, pl.ds(q * slice_width, slice_width)],
            x_buf.at[me, my_half],
            tok_rs.at[me],
        )

    def is_self(q):
        return tensor * per_tensor + q == me

    def token_share(source, off):
        return remote(
            x_buf.at[source, my_half],
            x_buf.at[source, my_half],
            ty_ss.at[source * tensors + off],
            tok_rs.at[source],
            {"tensor": lax.rem(tensor + off, tensors)},
        )

    for q in range(per_tensor):

        @pl.when(is_self(q))
        def _():
            token_local(q).start()

        @pl.when(jnp.logical_not(is_self(q)))
        def _():
            token_copy(q).start()

    def gain_copy(off):
        return remote(
            gain_ref.at[:, columns(lax.rem(me, per_tensor), slice_width)],
            gain_buf.at[core],
            gain_ss.at[off],
            gain_rs.at[core],
            place(lax.rem(member + off, group)),
        )

    gain_local = pltpu.make_async_copy(
        gain_ref.at[:, columns(lax.rem(me, per_tensor), slice_width)],
        gain_buf.at[core],
        gain_rs.at[core],
    )

    @pl.when(at_home)
    def _():
        gain_local.start()
        for off in range(1, group):
            gain_copy(off).start()

    def up_half(index):
        if up_ref.shape[0] == sections:
            return up_ref.at[index]
        return up_ref.at[0, :, columns(index, half)]

    give_up = remote(
        up_half(other),
        up_buf.at[core],
        w_ss.at[0],
        w_rs.at[0],
        {"section": other},
    )
    give_up.start()
    own_up = pltpu.make_async_copy(
        up_half(core), up_buf.at[core], own_sem.at[0]
    )
    own_up.start()

    cot_copies = []
    for m in range(1, dp_count):
        target = lax.rem(me + m, dp_count)
        copy = remote(
            cot_ref.at[0, my_part, columns(target, slice_width)],
            cot_buf.at[me, my_part],
            cot_ss.at[m],
            cot_rs.at[m],
            {"dp": target},
        )
        copy.start()
        cot_copies.append(copy)
    cot_local = pltpu.make_async_copy(
        cot_ref.at[0, my_part, columns(me, slice_width)], cot_buf.at[me, my_part], own_sem.at[2]
    )
    cot_local.start()

    give_down = remote(
        down_ref.at[0, columns(other, half), :],
        down_buf.at[core],
        w_ss.at[1],
        w_rs.at[1],
        {"section": other},
    )
    give_down.start()
    own_down = pltpu.make_async_copy(
        down_ref.at[0, columns(core, half), :], down_buf.at[core], own_sem.at[1]
    )
    own_down.start()

    def token_forward(source):
        return remote(
            x_buf.at[source, my_half],
            x_buf.at[source, my_half],
            tf_ss.at[source],
            tf_rs.at[source],
            {"section": other},
        )

    for source in range(dp_count):
        pltpu.make_async_copy(
            x_buf.at[source, my_half], x_buf.at[source, my_half], tok_rs.at[source]
        ).wait()

        @pl.when(at_home)
        def _():
            for off in range(1, tensors):
                token_share(source, off).start()

        token_forward(source).start()

    ends = []

    def put(src, dst):
        copy = pltpu.make_async_copy(src, dst, end_sem.at[len(ends)])
        copy.start()
        ends.append(copy)

    own_up.wait()
    give_up.wait_recv()
    put(up_buf.at[0], up_out0)
    put(up_buf.at[1], up_out1)
    own_down.wait()
    give_down.wait_recv()
    put(down_buf.at[0], down_out0)
    put(down_buf.at[1], down_out1)
    for layer in range(sections):
        pltpu.make_async_copy(
            gain_buf.at[layer], gain_buf.at[layer], gain_rs.at[layer]
        ).wait()
    put(gain_buf.at[0], gain_out0)
    put(gain_buf.at[1], gain_out1)

    def cot_share(m, off):
        source = lax.rem(me + dp_count - m, dp_count)
        return remote(
            cot_buf.at[source, my_part],
            cot_buf.at[source, my_part],
            cy_ss.at[m * tensors + off],
            cy_rs.at[m * tensors + off],
            {"tensor": lax.rem(tensor + off, tensors)},
        )

    for m in range(dp_count):
        if m == 0:
            cot_local.wait()
        else:
            cot_copies[m - 1].wait_recv()
        for off in range(1, tensors):
            cot_share(m, off).start()

    for source in range(dp_count):
        token_forward(source).wait_recv()
    put(x_buf, x_out)
    for m in range(dp_count):
        for off in range(1, tensors):
            cot_share(m, off).wait_recv()
    put(cot_buf, cot_out)

    for q in range(per_tensor):

        @pl.when(jnp.logical_not(is_self(q)))
        def _():
            token_copy(q).wait_send()

    @pl.when(at_home)
    def _():
        for off in range(1, group):
            gain_copy(off).wait_send()
        for source in range(dp_count):
            for off in range(1, tensors):
                token_share(source, off).wait_send()

    give_up.wait_send()
    give_down.wait_send()
    for copy in cot_copies:
        copy.wait_send()
    for source in range(dp_count):
        token_forward(source).wait_send()
    for m in range(dp_count):
        for off in range(1, tensors):
            cot_share(m, off).wait_send()
    for copy in ends:
        copy.wait()


def front(sizes, tokens, gain, w_up, w_down, cotangent):
    sections, dp_count, tensors = sizes
    assert sections == 2
    group = sections * tensors
    per_tensor = dp_count // tensors
    rows, own_width = tokens.shape
    slice_width = own_width // per_tensor
    depth = w_up.shape[1]
    half = w_up.shape[2] // sections
    dma = pltpu.SemaphoreType.DMA
    hbm = pl.BlockSpec(memory_space=pl.ANY)
    if half % 128:
        w_up = w_up[0].reshape(depth, sections, half).transpose(1, 0, 2)

    def shape(*dims, dtype=BF16):
        return jax.ShapeDtypeStruct(dims, dtype)

    return pl.pallas_call(
        functools.partial(front_kernel, sizes),
        name="front",
        out_shape=(
            shape(dp_count, rows, slice_width),
            shape(1, slice_width, dtype=F32),
            shape(1, slice_width, dtype=F32),
            shape(depth, half),
            shape(depth, half),
            shape(half, slice_width),
            shape(half, slice_width),
            shape(dp_count, rows, slice_width),
        ),
        in_specs=[hbm] * 5,
        out_specs=(hbm,) * 8,
        scratch_shapes=[
            pltpu.VMEM((dp_count, rows, slice_width), BF16),
            pltpu.VMEM((sections, 1, slice_width), F32),
            pltpu.VMEM((sections, depth, half), BF16),
            pltpu.VMEM((sections, half, slice_width), BF16),
            pltpu.VMEM((dp_count, rows, slice_width), BF16),
            dma((dp_count,)),
            dma((dp_count,)),
            dma((dp_count * tensors,)),
            dma((dp_count,)),
            dma((dp_count,)),
            dma((dp_count,)),
            dma((dp_count,)),
            dma((dp_count * tensors,)),
            dma((dp_count * tensors,)),
            dma((group,)),
            dma((sections,)),
            dma((2,)),
            dma((2,)),
            dma((3,)),
            dma((8,)),
        ],
        compiler_params=pltpu.CompilerParams(collective_id=sections, has_side_effects=True),
    )(tokens, gain.astype(F32), w_up, w_down, cotangent)


def body(tokens, gain, w_up, w_down, cotangent):
    core = lax.axis_index("section")
    layers = lax.axis_size("section")
    dp_count = lax.axis_size("dp")
    tensor_count = lax.axis_size("tensor")
    rows, own_width = tokens.shape
    width = own_width * tensor_count
    half = w_up.shape[2] // layers
    all_rows = rows * dp_count
    sizes = (layers, dp_count, tensor_count)

    def swap(array):
        return lax.ppermute(array, "section", [(0, 1), (1, 0)])

    def both(own, got):
        return (jnp.where(core == 0, own, got), jnp.where(core == 0, got, own))

    x, *rest = front(sizes, tokens, gain, w_up, w_down, cotangent)
    gains, up_parts, down_parts = rest[0:2], rest[2:4], rest[4:6]
    cot_mine = rest[6].reshape(all_rows, -1)

    states = []
    hiddens = []
    for layer in range(layers):
        hidden, x, state = layer_step(
            layer, sizes, width, x, gains[layer], up_parts[layer], down_parts[layer]
        )
        hiddens.append(hidden.reshape(all_rows, half))
        states.append(state)
    state = jnp.where(core == 0, states[0], states[1])

    hid_keep = jnp.where(core == 0, hiddens[0], hiddens[1])
    hid_got = swap(jnp.where(core == 0, hiddens[1], hiddens[0]))
    hid_parts = both(hid_keep, hid_got)
    hidden_whole = jnp.concatenate(hid_parts, axis=1)
    grad = lax.dot_general(
        hidden_whole, cot_mine, (((0,), (0,)), ((), ())), preferred_element_type=F32
    ).astype(BF16)
    return (state[None], grad[None])


def solution(mesh):
    placed = (
        P("dp", "tensor"),
        P("section", "tensor"),
        P("section", "dp", "tensor"),
        P("section", "tensor", "dp"),
        P("section", "dp", None),
    )
    return jax.shard_map(
        body,
        mesh=mesh,
        in_specs=placed,
        out_specs=(P("section", "dp", "tensor"), P("section", "tensor", "dp")),
        check_vma=False,
    )
```

profile of v0, /device:TPU:29, one launch (start us, length us, event | category | flops | bytes accessed | tf_op | source)
XLA Modules:
  0.0 310.2 jit_solution(6178584044114929735)
XLA Ops:
  0.6 1.3 convert_element_type.6.gain_ref
  1.9 1.1 copy.9
  3.0 0.9 copy.10
  4.0 77.0 %front.1 = (bf16[16,128,256]{2,1,0:T(8,128)(2,1)}, f32[1,256]{1,0:T(1,128)}, f32[1,256]{1,0:T(1,128)}, bf16[256,320]{1,0:T(8,128)(2,1)}, bf16[256,320]{1,0:T(8,1...) custom-call(bf16[128,512]{1,0:T(8,128)(2,1)} %tok_ref.1, ...), custom_call_target="tpu_custom_call" | custom-call | tf_op jit(solution)/shard_map/front/pallas_call | solution.py:782
  81.0 121.4 %layer0.1 = (bf16[16,128,320]{2,1,0:T(8,128)(2,1)}, bf16[16,128,256]{2,1,0:T(8,128)(2,1)}, bf16[128,512]{1,0:T(8,128)(2,1)}) custom-call(bf16[16,128,256]{2,1,0:T(8,128)(2,1)} %get-tuple-element.15.x_ref, f32[1,256]{1,0:T(1,128)} %get-tuple-element.16.gain_ref, bf16[256,320]{1,0:T(8,128)(2,1)} %get-tuple-element.17.up_ref, ...), custom_call_target="tpu_custom_call" | custom-call | tf_op jit(solution)/shard_map/layer0/pallas_call | solution.py:456
  202.4 97.5 %layer1.1 = (bf16[16,128,320]{2,1,0:T(8,128)(2,1)}, bf16[1,8,128]{2,1,0:T(8,128)(2,1)}, bf16[128,512]{1,0:T(8,128)(2,1)}) custom-call(bf16[16,128,256]{2,1,0:T(8,128)(2,1)} %get-tuple-element.20.x_ref, f32[1,256]{1,0:T(1,128)} %get-tuple-element.21.gain_ref, bf16[256,320]{1,0:T(8,128)(2,1)} %get-tuple-element.22.up_ref, ...), custom_call_target="tpu_custom_call" | custom-call | tf_op jit(solution)/shard_map/layer1/pallas_call | solution.py:456
  299.9 2.2 broadcast_select_fusion.1
  302.1 1.6 copy.11
  303.7 0.0 copy-start
  303.7 0.0 copy-start.1
  303.7 0.0 collective-permute-start
  303.7 0.7 copy.12
  304.4 0.2 copy-done
  304.6 0.1 copy-done.1
  304.7 0.7 select_bitcast_fusion
  305.3 0.0 copy-start.2
  305.3 1.7 collective-permute-done
  307.1 1.5 broadcast_select_fusion.3
  308.6 0.0 copy-done.2
  308.6 1.6 fusion.7
Async XLA Ops:
  303.7 0.9 copy-start
  303.7 1.0 copy-start.1
  303.7 3.4 %collective-permute-start = (bf16[2048,320]{0,1:T(8,128)(2,1)}, bf16[2048,320]{0,1:T(8,128)(2,1)}, u32[]{:S(2)}, u32[]{:S(2)}) collective-permute-start(bf16[2048,320]{0,1:T(8,128)(2,1)} %copy.11), channel_id=1, source_target_pairs={{0,128},{128,0},{1,129},{129,1},{2,130},{130,2},{3,131},{131,3},{4... | collective-permute-start | bytes 3932168 | tf_op jit(solution)/shard_map/ppermute | solution.py:835
  305.3 3.2 %copy-start.2 = (bf16[16,128,256]{2,1,0:T(8,128)(2,1)S(1)}, bf16[16,128,256]{2,1,0:T(8,128)(2,1)}, u32[]{:S(2)}) copy-start(bf16[16,128,256]{2,1,0:T(8,128)(2,1)} %get-tuple-element.27) | copy-start | bytes 3145732
where the time goes:
time: 310 us
  Pallas kernels  296 us (95%)
  other arithmetic  5.6 us (2%)
  local copies, waits for them, and re-layouts  4.6 us (1%)
    pallas_call x2, Pallas kernels, layer_step(): pl.pallas_call(functools.partial(layer_kernel, sizes, inner, width, layer...  219 us
    pallas_call x1, Pallas kernels, front(): pl.pallas_call(functools.partial(front_kernel, sizes), name='front', out_...  77 us
  transfers between devices with their start and end apart: 1, of which 1 were waited for; matrix products, arithmetic and copies ran while one was open for 0% of the time, Pallas kernels for 0%

commit v1 on v0

v1 whole, which is shorter than its diff:
```python
import functools

import jax
import jax.numpy as jnp
from jax import lax
from jax.experimental import pallas as pl
from jax.experimental.pallas import tpu as pltpu
from jax.sharding import PartitionSpec as P

EPS = 1e-06
F32 = jnp.float32
BF16 = jnp.bfloat16

MESH = pl.DeviceIdType.MESH
LANES = 128
PIECES = 2
INNER = 2


def far_first(count):
    return sorted(range(1, count), key=lambda k: abs(2 * k - count))


def remote(src, dst, send_sem, recv_sem, target):
    return pltpu.make_async_remote_copy(
        src_ref=src,
        dst_ref=dst,
        send_sem=send_sem,
        recv_sem=recv_sem,
        device_id=target,
        device_id_type=MESH,
    )


def stack_kernel(
    sizes,
    width,
    tok_ref,
    gain_ref,
    up_ref,
    down_ref,
    cot_ref,
    state_out,
    grad_out,
    tok,
    gain_f,
    gains,
    wu,
    wd,
    xb,
    xg,
    ssq,
    acc,
    sq_send,
    sq_recv,
    up_send,
    up_recv,
    hid,
    part_send,
    part_recv,
    state_buf,
    hg,
    cb,
    gacc,
    gsend,
    grecv,
    ld,
    tk_ss,
    tk_rs,
    ga_ss,
    ga_rs,
    z_ss,
    z_rs,
    f_ss,
    f_rs,
    c_ss,
    c_rs,
    cs_ss,
    cs_rs,
    sq_ss,
    sq_rs,
    ux_ss,
    ux_rs,
    ax_ss,
    ax_rs,
    hd_ss,
    hd_rs,
    h_ss,
    h_rs,
    p_ss,
    p_rs,
    x_ss,
    x_rs,
    st_ss,
    st_rs,
    gx_ss,
    gx_rs,
    end_sem,
):
    sections, dp_count, nt = sizes
    nz = dp_count // INNER
    hi = nz // 2
    lo = nz - 1 - hi
    rows, slice_width = tok.shape
    h2 = rows // sections
    feat = slice_width // INNER
    part_rows = rows // nt
    hidden = wu.shape[3]

    core = lax.axis_index("section")
    t = lax.axis_index("tensor")
    me = lax.axis_index("dp")
    z = me // INNER
    q = lax.rem(me, INNER)
    other = 1 - core
    sign = 1 - 2 * core
    beside = z * INNER + 1 - q

    def block_of(index, size):
        return pl.ds(pl.multiple_of(index * size, size), size)

    mine = block_of(q, h2)
    theirs = block_of(1 - q, h2)
    core_rows = block_of(core, h2)
    other_rows = block_of(other, h2)
    my_cols = block_of(q, feat)
    their_cols = block_of(1 - q, feat)
    my_part = block_of(t, part_rows)

    def tensor_at(off):
        return lax.rem(t + off, nt)

    def plane_at(shift):
        return lax.rem(z + nz + shift, nz)

    sends = []

    def launch(make, *args, cond=None):
        make = functools.partial(make, *args)
        sends.append((make, cond))
        if cond is None:
            make().start()
        else:
            pl.when(cond())(lambda: make().start())

    loads = [
        pltpu.make_async_copy(up_ref.at[0], wu.at[core, z], ld.at[0]),
        pltpu.make_async_copy(tok_ref, tok, ld.at[1]),
        pltpu.make_async_copy(down_ref.at[0], wd.at[core, z], ld.at[2]),
        pltpu.make_async_copy(
            cot_ref.at[0, my_part, block_of(z, slice_width)], cb.at[z, my_part], ld.at[3]
        ),
    ]
    for copy in loads:
        copy.start()

    barrier = pltpu.get_barrier_semaphore()

    def greet(target):
        pl.semaphore_signal(barrier, inc=1, device_id=target, device_id_type=MESH)

    for m in far_first(nz):
        greet({"dp": plane_at(m) * INNER + q})
    for off in far_first(nt) + [0]:
        greet({"dp": beside, "tensor": tensor_at(off)})
        greet({"section": other, "tensor": tensor_at(off)})
        if off:
            greet({"tensor": tensor_at(off)})
    greet({"section": other, "dp": beside})

    gain_f[...] = gain_ref[...].astype(F32)
    gains[core, t] = gain_f[:, my_cols]
    ssq[...] = jnp.zeros_like(ssq)
    for copy in loads:
        copy.wait()
    xb[0, t, mine] = tok[core_rows, my_cols]

    pl.semaphore_wait(barrier, (nz - 1) + (2 * nt - 1) + nt + 1)

    def weight(layer, kind, origin, piece):
        buf = wd if kind else wu
        size = buf.shape[2] // PIECES
        return buf.at[layer, origin, pl.ds(piece * size, size)]

    def along(d):
        return plane_at(-sign * d)

    def against(d):
        return plane_at(sign * d)

    def hop(m, piece, s):
        ref = weight(m // 2, m % 2, along(s), piece)
        return remote(
            ref,
            ref,
            z_ss.at[m, piece, s],
            z_rs.at[m, piece, s],
            {"dp": plane_at(sign) * INNER + q},
        )

    def landing(m, piece, d):
        ref = weight(m // 2, m % 2, along(d), piece)
        return remote(
            ref,
            ref,
            z_ss.at[m, piece, d - 1],
            z_rs.at[m, piece, d - 1],
            {"dp": plane_at(sign) * INNER + q},
        )

    def push(m, piece, d):
        ref = weight(m // 2, m % 2, along(d), piece)
        return remote(
            ref, ref, f_ss.at[m, piece, d], f_rs.at[m, piece, d], {"section": other}
        )

    def pushed(m, piece, d):
        ref = weight(m // 2, m % 2, against(d), piece)
        return remote(
            ref, ref, f_ss.at[m, piece, d], f_rs.at[m, piece, d], {"section": other}
        )

    def push_own(kind, piece):
        ref = weight(core, kind, z, piece)
        m = 2 * core + kind
        return remote(
            ref, ref, f_ss.at[m, piece, 0], f_rs.at[m, piece, 0], {"section": other}
        )

    def holds(layer):
        return lambda: core == layer

    def lacks(layer):
        return lambda: core != layer

    def pass_on(m, piece, s):
        if s < lo:
            launch(hop, m, piece, s)
        elif s < hi:
            launch(hop, m, piece, s, cond=holds(m // 2))

    def advance(m, d):
        layer = m // 2
        for piece in range(PIECES):
            if d == 0:

                @pl.when(core != layer)
                def _():
                    pushed(m, piece, 0).wait_recv()

                pass_on(m, piece, 0)
            elif d <= lo:
                landing(m, piece, d).wait_recv()
                pass_on(m, piece, d)
                launch(push, m, piece, d)
            else:

                @pl.when(core == layer)
                def _():
                    landing(m, piece, d).wait_recv()

                launch(push, m, piece, d, cond=holds(layer))

    def take(m, d):
        for piece in range(PIECES):
            pushed(m, piece, d).wait_recv()

    def take_far(m):
        @pl.when(core != m // 2)
        def _():
            take(m, hi)

    for piece in range(PIECES):
        launch(push_own, 0, piece)

    @pl.when(core == 0)
    def _():
        for piece in range(PIECES):
            hop(0, piece, 0).start()

    def token_copy(away, off):
        cols, dp = (their_cols, beside) if away else (my_cols, me)
        return remote(
            tok.at[core_rows, cols],
            xb.at[0, t, mine],
            tk_ss.at[away, off],
            tk_rs.at[t, q],
            {"dp": dp, "tensor": tensor_at(off)},
        )

    def token_landing(tensor, cls):
        ref = xb.at[0, tensor, block_of(cls, h2)]
        return remote(ref, ref, tk_ss.at[0, 0], tk_rs.at[tensor, cls], {"dp": beside})

    for off in far_first(nt) + [0]:
        launch(token_copy, 1, off)
        if off:
            launch(token_copy, 0, off)

    def gain_copy(away, off):
        return remote(
            gains.at[core, t],
            gains.at[core, t],
            ga_ss.at[away, off],
            ga_rs.at[core, t],
            {"section": other if away else core, "tensor": tensor_at(off)},
        )

    def gain_landing(layer, tensor):
        ref = gains.at[layer, tensor]
        return remote(ref, ref, ga_ss.at[0, 0], ga_rs.at[layer, tensor], {"section": other})

    for off in far_first(nt) + [0]:
        launch(gain_copy, 1, off)
        if off:
            launch(gain_copy, 0, off)
    for piece in range(PIECES):
        launch(push_own, 1, piece)

    def cot_copy(m):
        to = plane_at(m)
        return remote(
            cot_ref.at[0, my_part, block_of(to, slice_width)],
            cb.at[z, my_part],
            c_ss.at[m],
            c_rs.at[z],
            {"dp": to * INNER + q},
        )

    def cot_landing(origin):
        ref = cb.at[origin, my_part]
        return remote(ref, ref, c_ss.at[0], c_rs.at[origin], {"dp": beside})

    @pl.when(core != 0)
    def _():
        for piece in range(PIECES):
            pushed(0, piece, 0).wait_recv()
            if lo:
                hop(0, piece, 0).start()

    for piece in range(PIECES):
        sends.append((functools.partial(hop, 0, piece, 0), None if lo else holds(0)))
    for m in far_first(nz):
        launch(cot_copy, m)

    def cot_share(off):
        ref = cb.at[:, my_part]
        return remote(ref, ref, cs_ss.at[off], cs_rs.at[t], {"tensor": tensor_at(off)})

    def cot_share_landing(tensor):
        ref = cb.at[:, block_of(tensor, part_rows)]
        return remote(ref, ref, cs_ss.at[0], cs_rs.at[tensor], {"dp": beside})

    def share_cotangent():
        for m in range(1, nz):
            cot_landing(plane_at(m)).wait_recv()
        for off in far_first(nt):
            launch(cot_share, off)

    def prepare(layer, block):
        x = xb[layer, block].astype(F32)
        xg[block] = (x * gains[layer, block]).astype(BF16)
        square = x * x
        total = ssq[...]
        for lower in range(0, feat, LANES):
            total = total + square[:, lower : lower + LANES]
        ssq[...] = total

    def up_block(layer, block, first=False):
        value = jnp.dot(xg[block], wu[layer, block], preferred_element_type=F32)
        acc[...] = value if first else acc[...] + value

    def sum_copy(layer):
        return remote(
            sq_send.at[layer], sq_recv.at[layer], sq_ss.at[layer], sq_rs.at[layer], {"dp": beside}
        )

    def send_sums(layer):
        sq_send[layer] = jnp.broadcast_to(
            jnp.sum(ssq[theirs], axis=1, keepdims=True), (h2, LANES)
        )
        launch(sum_copy, layer)

    def up_copy(layer):
        return remote(
            up_send.at[layer], up_recv.at[layer], ux_ss.at[layer], ux_rs.at[layer], {"dp": beside}
        )

    def send_up(layer):
        up_send[layer] = acc[theirs].astype(BF16)
        launch(up_copy, layer)

    def hidden_copy(layer):
        ref = hid.at[layer, mine]
        return remote(ref, ref, ax_ss.at[layer], ax_rs.at[layer], {"dp": beside})

    def hidden_landing(layer):
        ref = hid.at[layer, theirs]
        return remote(ref, ref, ax_ss.at[layer], ax_rs.at[layer], {"dp": beside})

    def hidden_give(layer):
        return remote(
            hid.at[layer, mine],
            hg.at[z, core_rows],
            hd_ss.at[layer],
            hd_rs.at[layer],
            {"section": other},
        )

    def hidden_given(layer):
        ref = hg.at[z, other_rows]
        return remote(ref, ref, hd_ss.at[layer], hd_rs.at[layer], {"section": other})

    def finish_up(layer):
        sum_copy(layer).wait_recv()
        total = jnp.sum(ssq[mine], axis=1, keepdims=True) + sq_recv[layer]
        inverse = lax.rsqrt(total / width + EPS)
        up_copy(layer).wait_recv()
        for lower in range(0, hidden, LANES):
            cols = pl.ds(lower, LANES)
            value = (acc[mine, cols] + up_recv[layer, :, cols].astype(F32)) * inverse
            hid[layer, mine, cols] = jax.nn.gelu(value, approximate=True).astype(BF16)
        launch(hidden_copy, layer)
        launch(hidden_give, layer, cond=lacks(layer))

        @pl.when(core == layer)
        def _():
            hg[z, core_rows] = hid[layer, mine]

        if layer == 0:
            ssq[...] = jnp.zeros_like(ssq)

    def ring_length(k, way):
        return hi if k == way else lo

    def ring_copy(k, way, s, layer):
        delta = 1 if way == 0 else -1
        ref = hg.at[plane_at(-delta * s), block_of(layer if k == 0 else 1 - layer, h2)]
        return remote(
            ref,
            ref,
            h_ss.at[k, way, s],
            h_rs.at[k, way, s],
            {"dp": plane_at(delta) * INNER + q},
        )

    def ring_landing(k, way, d, layer):
        delta = 1 if way == 0 else -1
        ref = hg.at[plane_at(-delta * d), block_of(layer if k == 0 else 1 - layer, h2)]
        return remote(
            ref,
            ref,
            h_ss.at[k, way, d - 1],
            h_rs.at[k, way, d - 1],
            {"dp": plane_at(delta) * INNER + q},
        )

    def ring_step(layer, d):
        @pl.when(core == layer)
        def _():
            for k in range(2):
                if d == 0 and k == 1:
                    hidden_given(layer).wait_recv()
                for way in range(2):
                    length = ring_length(k, way)
                    if 0 < d <= length:
                        ring_landing(k, way, d, layer).wait_recv()
                    if d < length:
                        ring_copy(k, way, d, layer).start()

    def part_copy(layer, block):
        return remote(
            part_send.at[layer, block],
            part_recv.at[layer, t],
            p_ss.at[layer, block],
            p_rs.at[layer, t],
            {"tensor": block},
        )

    def part_landing(layer, tensor):
        ref = part_recv.at[layer, tensor]
        return remote(
            ref, ref, p_ss.at[layer, tensor], p_rs.at[layer, tensor], {"tensor": tensor}
        )

    def down_block(layer, block):
        part_send[layer, block] = jnp.dot(
            hid[layer], wd[layer, block], preferred_element_type=F32
        ).astype(BF16)

        @pl.when(block != t)
        def _():
            part_copy(layer, block).start()

    def next_copy(off):
        ref = xb.at[1, t]
        return remote(ref, ref, x_ss.at[off], x_rs.at[t], {"tensor": tensor_at(off)})

    def next_landing(tensor):
        ref = xb.at[1, tensor]
        return remote(ref, ref, x_ss.at[0], x_rs.at[tensor], {"tensor": tensor})

    def state_copy(layer, away):
        return remote(
            xb.at[layer + 1, t, theirs if away else mine],
            state_buf.at[core_rows, my_cols],
            st_ss.at[layer, away],
            st_rs.at[core, q],
            {"section": layer, "dp": beside} if away else {"section": other},
        )

    def state_landing(from_core, from_class):
        ref = state_buf.at[block_of(from_core, h2), block_of(from_class, feat)]
        return remote(
            ref, ref, st_ss.at[0, 0], st_rs.at[from_core, from_class], {"section": other}
        )

    def finish_down(layer):
        value = xb[layer, t].astype(F32) + part_send[layer, t].astype(F32)
        for off in range(1, nt):
            tensor = tensor_at(off)
            part_landing(layer, tensor).wait_recv()
            value = value + part_recv[layer, tensor].astype(F32)
        xb[layer + 1, t] = value.astype(BF16)
        if layer == 0:
            for off in far_first(nt):
                launch(next_copy, off)
        launch(state_copy, layer, 1)
        launch(state_copy, layer, 0, cond=lacks(layer))

        @pl.when(core == layer)
        def _():
            state_buf[core_rows, my_cols] = xb[layer + 1, t, mine]

    def grad_block(origin, first=False):
        left = hg[origin]
        for index, cols in ((0, their_cols), (1, my_cols)):
            value = lax.dot_general(
                left, cb[origin, :, cols], (((0,), (0,)), ((), ())), preferred_element_type=F32
            )
            gacc[index] = value if first else gacc[index] + value

    def grad_copy():
        return remote(gsend, grecv, gx_ss.at[0], gx_rs.at[0], {"dp": beside})

    advance(0, 1)
    if hi >= 2:
        advance(0, 2)
    for off in range(nt):
        tensor = tensor_at(off)
        token_landing(tensor, 1 - q).wait_recv()
        if off:
            token_landing(tensor, q).wait_recv()
            gain_landing(core, tensor).wait_recv()
        gain_landing(other, tensor).wait_recv()

    def prepare_first(block, carry):
        prepare(0, block)
        return carry

    lax.fori_loop(0, nt, prepare_first, 0)
    send_sums(0)
    share_cotangent()

    def use_near(m, d, use):
        use(along(d))
        take(m, d)
        use(against(d))

    def use_far(m, use):
        take_far(m)
        use(along(hi))

    up0 = functools.partial(up_block, 0)
    up_block(0, z, first=True)
    if lo >= 1:
        use_near(0, 1, up0)
    for d in range(3, hi + 1):
        advance(0, d)
        if d == hi:
            advance(1, 0)
        use_near(0, d - 1, up0)
    if hi < 3:
        advance(1, 0)
        for d in range(2, lo + 1):
            use_near(0, d, up0)
    use_far(0, up0)
    send_up(0)
    if hi >= 2:
        advance(1, 1)
    finish_up(0)
    for d in range(2, hi):
        advance(1, d)
    advance(2, 0)
    down0 = functools.partial(down_block, 0)
    hidden_landing(0).wait_recv()
    down_block(0, z)
    for d in range(1, lo):
        use_near(1, d, down0)
    advance(1, hi)
    if lo >= 1:
        use_near(1, lo, down0)
    use_far(1, down0)
    advance(2, 1)
    ring_step(0, 0)
    if hi >= 2:
        advance(2, 2)
    finish_down(0)
    ring_step(0, 1)
    for d in range(3, hi + 1):
        advance(2, d)
    advance(3, 0)
    for d in range(2, hi + 1):
        ring_step(0, d)

    prepare(1, t)
    for d in range(1, lo + 1):
        take(2, d)
    take_far(2)
    up_block(1, t, first=True)
    for count, off in enumerate(reversed(far_first(nt))):
        if count == nt // 2 - 1:
            advance(3, 1)
        tensor = tensor_at(off)
        next_landing(tensor).wait_recv()
        prepare(1, tensor)
        up_block(1, tensor)
    send_sums(1)
    send_up(1)
    if hi >= 2:
        advance(3, 2)
    finish_up(1)
    ring_step(1, 0)
    for d in range(3, hi + 1):
        advance(3, d)
    hidden_landing(1).wait_recv()
    down1 = functools.partial(down_block, 1)
    down_block(1, z)
    for d in range(1, lo + 1):
        use_near(3, d, down1)
    use_far(3, down1)

    for off in range(1, nt):
        cot_share_landing(tensor_at(off)).wait_recv()

    grad_block(z, first=True)
    for d in range(1, hi + 1):
        ring_step(1, d)
        if d <= lo:

            def both(i, carry):
                grad_block(plane_at(d - 2 * d * i))
                return carry

            lax.fori_loop(0, 2, both, 0)
        else:
            grad_block(plane_at(d))
    gsend[...] = gacc[0].astype(BF16)
    grad_copy().start()
    finish_down(1)
    state_landing(other, q).wait_recv()
    state_landing(core, 1 - q).wait_recv()
    state_landing(other, 1 - q).wait_recv()
    state_store = pltpu.make_async_copy(state_buf, state_out, end_sem.at[0])
    state_store.start()
    grad_copy().wait_recv()
    grad_copy().wait_send()
    gsend[...] = (gacc[1] + grecv[...].astype(F32)).astype(BF16)
    grad_store = pltpu.make_async_copy(gsend, grad_out, end_sem.at[1])
    grad_store.start()

    for make, cond in sends:
        if cond is None:
            make().wait_send()
        else:
            pl.when(cond())(lambda: make().wait_send())
    for layer in range(sections):
        for block in range(nt):

            @pl.when(block != t)
            def _():
                part_copy(layer, block).wait_send()

    for k in range(2):
        for way in range(2):
            for s in range(ring_length(k, way)):
                ring_copy(k, way, s, core).wait_send()
    state_store.wait()
    grad_store.wait()


def stack(sizes, tokens, gain, w_up, w_down, cotangent):
    sections, dp_count, nt = sizes
    nz = dp_count // INNER
    assert sections == 2 and nz == nt and nz % 2 == 0
    rows, slice_width = tokens.shape
    feat = slice_width // INNER
    h2 = rows // sections
    hidden = w_up.shape[2]
    assert w_up.shape[1] == feat and w_down.shape[2] == feat
    width = slice_width * nt
    hi = nz // 2
    dma = pltpu.SemaphoreType.DMA
    hbm = pl.BlockSpec(memory_space=pl.ANY)
    vmem = pl.BlockSpec(memory_space=pltpu.VMEM)

    def buf(*dims, dtype=BF16):
        return pltpu.VMEM(dims, dtype)

    def pair(*dims):
        return [dma(dims)] * 2

    return pl.pallas_call(
        functools.partial(stack_kernel, sizes, width),
        name="stack",
        out_shape=(
            jax.ShapeDtypeStruct((rows, slice_width), BF16),
            jax.ShapeDtypeStruct((hidden, feat), BF16),
        ),
        in_specs=[hbm, vmem, hbm, hbm, hbm],
        out_specs=(hbm, hbm),
        scratch_shapes=[
            buf(rows, slice_width),
            buf(1, slice_width, dtype=F32),
            buf(sections, nt, 1, feat, dtype=F32),
            buf(sections, nz, feat, hidden),
            buf(sections, nz, hidden, feat),
            buf(sections + 1, nt, rows, feat),
            buf(nt, rows, feat),
            buf(rows, LANES, dtype=F32),
            buf(rows, hidden, dtype=F32),
            buf(sections, h2, LANES, dtype=F32),
            buf(sections, h2, LANES, dtype=F32),
            buf(sections, h2, hidden),
            buf(sections, h2, hidden),
            buf(sections, rows, hidden),
            buf(sections, nt, rows, feat),
            buf(sections, nt, rows, feat),
            buf(rows, slice_width),
            buf(nz, rows, hidden),
            buf(nz, rows, slice_width),
            buf(2, hidden, feat, dtype=F32),
            buf(hidden, feat),
            buf(hidden, feat),
            dma((4,)),
            dma((2, nt)),
            dma((nt, INNER)),
            dma((2, nt)),
            dma((sections, nt)),
        ]
        + pair(2 * sections, PIECES, hi)
        + pair(2 * sections, PIECES, hi + 1)
        + pair(nz)
        + pair(nt)
        + pair(sections) * 4
        + pair(2, 2, hi)
        + pair(sections, nt)
        + pair(nt)
        + [dma((sections, 2)), dma((sections, INNER))]
        + pair(1)
        + [dma((2,))],
        compiler_params=pltpu.CompilerParams(collective_id=0, has_side_effects=True),
    )(tokens, gain, w_up, w_down, cotangent)


def body(tokens, gain, w_up, w_down, cotangent):
    sizes = (lax.axis_size("section"), lax.axis_size("dp"), lax.axis_size("tensor"))
    state, grad = stack(sizes, tokens, gain, w_up, w_down, cotangent)
    return (state[None], grad[None])


def solution(mesh):
    placed = (
        P("dp", "tensor"),
        P("section", "tensor"),
        P("section", "dp", "tensor"),
        P("section", "tensor", "dp"),
        P("section", "dp", None),
    )
    return jax.shard_map(
        body,
        mesh=mesh,
        in_specs=placed,
        out_specs=(P("section", "dp", "tensor"), P("section", "tensor", "dp")),
        check_vma=False,
    )
```

time: 310 us -> 121 us (0.39)
  the two profiles are of different devices: /device:TPU:29 before, /device:TPU:1 now
where the time goes in v1:
time: 121 us
  Pallas kernels  117 us (97%)
  local copies, waits for them, and re-layouts  3.29 us (3%)
    pallas_call x1, Pallas kernels, stack(): pl.pallas_call(functools.partial(stack_kernel, sizes, width), name='stack...  117 us
    unnamed x2, local copies, waits for them, and re-layouts  3.29 us

profile of v1, /device:TPU:1, one launch (start us, length us, event | category | flops | bytes accessed | tf_op | source)
XLA Modules:
  0.0 121.0 jit_solution(10045191982416106337)
XLA Ops:
  0.6 117.0 %stack.1 = (bf16[128,512]{1,0:T(8,128)(2,1)}, bf16[640,256]{1,0:T(8,128)(2,1)}) custom-call(bf16[128,512]{1,0:T(8,128)(2,1)} %tok_ref.1, bf16[1,512]{1,0:T(2,128)(2,1)} %gain_ref.1, bf16[1,256,640]{2,1,0:T(8,128)(2,1)} %up_ref.1, bf16[1,640,256]{2,1,0:T(8,128)(2,1)} %down_ref.1, bf16[1,128,4096]{2,1,0:T(8,128)(2,1)} %cot_ref.1), custom_call_target="tpu_custom_call" | custom-call | tf_op jit(solution)/shard_map/stack/pallas_call | solution.py:713
  117.7 1.6 %copy.9 = bf16[1,128,512]{2,1,0:T(8,128)(2,1)} copy(bf16[1,128,512]{2,1,0:T(8,128)(2,1)} %bitcast.3) | data formatting | bytes 262144
  119.2 1.7 %copy.10 = bf16[1,640,256]{2,1,0:T(8,128)(2,1)} copy(bf16[1,640,256]{2,1,0:T(8,128)(2,1)} %bitcast.2) | data formatting | bytes 655360

commit v2 on v1

--- a/solution.py
+++ b/solution.py
@@ -13,7 +13,7 @@
 
 MESH = pl.DeviceIdType.MESH
 LANES = 128
-PIECES = 2
+PIECES = 4
 INNER = 2
 
 
@@ -117,6 +117,8 @@
     beside = z * INNER + 1 - q
 
     def block_of(index, size):
+        if isinstance(index, int):
+            return pl.ds(index * size, size)
         return pl.ds(pl.multiple_of(index * size, size), size)
 
     mine = block_of(q, h2)
@@ -179,8 +181,7 @@
 
     def weight(layer, kind, origin, piece):
         buf = wd if kind else wu
-        size = buf.shape[2] // PIECES
-        return buf.at[layer, origin, pl.ds(piece * size, size)]
+        return buf.at[layer, origin, block_of(piece, buf.shape[2] // PIECES)]
 
     def along(d):
         return plane_at(-sign * d)
@@ -227,55 +228,59 @@
             ref, ref, f_ss.at[m, piece, 0], f_rs.at[m, piece, 0], {"section": other}
         )
 
-    def holds(layer):
-        return lambda: core == layer
-
     def lacks(layer):
         return lambda: core != layer
 
-    def pass_on(m, piece, s):
-        if s < lo:
-            launch(hop, m, piece, s)
-        elif s < hi:
-            launch(hop, m, piece, s, cond=holds(m // 2))
+    half = PIECES // 2
+    far_pieces = [core * half + j for j in range(half)]
+    near_pieces = [other * half + j for j in range(half)]
+
+    def begin(m):
+        for piece in range(PIECES):
+
+            @pl.when(core != m // 2)
+            def _():
+                pushed(m, piece, 0).wait_recv()
+
+        for piece in range(PIECES) if lo else far_pieces:
+            launch(hop, m, piece, 0)
 
     def advance(m, d):
-        layer = m // 2
-        for piece in range(PIECES):
-            if d == 0:
-
-                @pl.when(core != layer)
-                def _():
-                    pushed(m, piece, 0).wait_recv()
-
-                pass_on(m, piece, 0)
-            elif d <= lo:
+        for piece in range(PIECES) if d < lo else far_pieces:
+            landing(m, piece, d).wait_recv()
+            if d < hi:
+                launch(hop, m, piece, d)
+            launch(push, m, piece, d)
+        if d == max(lo, 1) and m + 1 < 2 * sections:
+            begin(m + 1)
+        if d == lo:
+            for piece in near_pieces:
                 landing(m, piece, d).wait_recv()
-                pass_on(m, piece, d)
                 launch(push, m, piece, d)
-            else:
-
-                @pl.when(core == layer)
-                def _():
-                    landing(m, piece, d).wait_recv()
-
-                launch(push, m, piece, d, cond=holds(layer))
+
+    rounds = [(m, d) for m in range(2 * sections) for d in range(1, hi + 1)]
+    done_rounds = [0]
+
+    def z_until(m, d):
+        last = rounds.index((m, min(d, hi))) + 1
+        for r in range(done_rounds[0], last):
+            advance(*rounds[r])
+        done_rounds[0] = max(done_rounds[0], last)
 
     def take(m, d):
         for piece in range(PIECES):
             pushed(m, piece, d).wait_recv()
 
     def take_far(m):
-        @pl.when(core != m // 2)
-        def _():
-            take(m, hi)
+        for piece in near_pieces:
+            pushed(m, piece, hi).wait_recv()
 
     for piece in range(PIECES):
         launch(push_own, 0, piece)
 
     @pl.when(core == 0)
     def _():
-        for piece in range(PIECES):
+        for piece in range(PIECES) if lo else far_pieces:
             hop(0, piece, 0).start()
 
     def token_copy(away, off):
@@ -335,11 +340,11 @@
     def _():
         for piece in range(PIECES):
             pushed(0, piece, 0).wait_recv()
-            if lo:
-                hop(0, piece, 0).start()
-
-    for piece in range(PIECES):
-        sends.append((functools.partial(hop, 0, piece, 0), None if lo else holds(0)))
+        for piece in range(PIECES) if lo else far_pieces:
+            hop(0, piece, 0).start()
+
+    for piece in range(PIECES) if lo else far_pieces:
+        sends.append((functools.partial(hop, 0, piece, 0), None))
     for m in far_first(nz):
         launch(cot_copy, m)
 
@@ -351,10 +356,12 @@
         ref = cb.at[:, block_of(tensor, part_rows)]
         return remote(ref, ref, cs_ss.at[0], cs_rs.at[tensor], {"dp": beside})
 
-    def share_cotangent():
+    def await_cotangent():
         for m in range(1, nz):
             cot_landing(plane_at(m)).wait_recv()
-        for off in far_first(nt):
+
+    def share_cotangent(first, last):
+        for off in far_first(nt)[first:last]:
             launch(cot_share, off)
 
     def prepare(layer, block):
@@ -543,9 +550,7 @@
     def grad_copy():
         return remote(gsend, grecv, gx_ss.at[0], gx_rs.at[0], {"dp": beside})
 
-    advance(0, 1)
-    if hi >= 2:
-        advance(0, 2)
+    z_until(0, 2)
     for off in range(nt):
         tensor = tensor_at(off)
         token_landing(tensor, 1 - q).wait_recv()
@@ -560,7 +565,6 @@
 
     lax.fori_loop(0, nt, prepare_first, 0)
     send_sums(0)
-    share_cotangent()
 
     def use_near(m, d, use):
         use(along(d))
@@ -573,44 +577,37 @@
 
     up0 = functools.partial(up_block, 0)
     up_block(0, z, first=True)
-    if lo >= 1:
-        use_near(0, 1, up0)
-    for d in range(3, hi + 1):
-        advance(0, d)
-        if d == hi:
-            advance(1, 0)
-        use_near(0, d - 1, up0)
-    if hi < 3:
-        advance(1, 0)
-        for d in range(2, lo + 1):
-            use_near(0, d, up0)
+    for d in range(1, lo + 1):
+        z_until(0, d + 1)
+        use_near(0, d, up0)
+    z_until(0, hi)
     use_far(0, up0)
     send_up(0)
-    if hi >= 2:
-        advance(1, 1)
+    await_cotangent()
+    z_until(1, 1)
     finish_up(0)
-    for d in range(2, hi):
-        advance(1, d)
-    advance(2, 0)
+    share_cotangent(0, nt // 2 - 1)
+    z_until(1, hi)
     down0 = functools.partial(down_block, 0)
     hidden_landing(0).wait_recv()
     down_block(0, z)
-    for d in range(1, lo):
+    for d in range(1, lo + 1):
         use_near(1, d, down0)
-    advance(1, hi)
-    if lo >= 1:
-        use_near(1, lo, down0)
     use_far(1, down0)
-    advance(2, 1)
     ring_step(0, 0)
-    if hi >= 2:
-        advance(2, 2)
+    z_until(2, 1)
+    if hi > 1:
+        ring_step(0, 1)
+    z_until(2, 2)
+    if hi > 2:
+        ring_step(0, 2)
     finish_down(0)
-    ring_step(0, 1)
-    for d in range(3, hi + 1):
-        advance(2, d)
-    advance(3, 0)
-    for d in range(2, hi + 1):
+    share_cotangent(nt // 2 - 1, nt)
+    z_until(2, 3)
+    if hi > 3:
+        ring_step(0, 3)
+    z_until(2, hi)
+    for d in range(max(1, min(4, hi)), hi + 1):
         ring_step(0, d)
 
     prepare(1, t)
@@ -618,21 +615,35 @@
         take(2, d)
     take_far(2)
     up_block(1, t, first=True)
-    for count, off in enumerate(reversed(far_first(nt))):
-        if count == nt // 2 - 1:
-            advance(3, 1)
+    for off in reversed(far_first(nt)):
         tensor = tensor_at(off)
         next_landing(tensor).wait_recv()
         prepare(1, tensor)
         up_block(1, tensor)
     send_sums(1)
     send_up(1)
-    if hi >= 2:
-        advance(3, 2)
+    z_until(3, 1)
+    for off in range(1, nt):
+        cot_share_landing(tensor_at(off)).wait_recv()
+
+    @pl.when(core == 0)
+    def _():
+        grad_block(z, first=True)
+
+        def one(i, carry):
+            grad_block(plane_at(i))
+            return carry
+
+        lax.fori_loop(1, nz, one, 0)
+        gsend[...] = gacc[0].astype(BF16)
+
+    z_until(3, 2)
     finish_up(1)
+    pl.when(core == 0)(lambda: grad_copy().start())
     ring_step(1, 0)
-    for d in range(3, hi + 1):
-        advance(3, d)
+    z_until(3, hi)
+    if hi > 1:
+        ring_step(1, 1)
     hidden_landing(1).wait_recv()
     down1 = functools.partial(down_block, 1)
     down_block(1, z)
@@ -640,13 +651,10 @@
         use_near(3, d, down1)
     use_far(3, down1)
 
-    for off in range(1, nt):
-        cot_share_landing(tensor_at(off)).wait_recv()
-
-    grad_block(z, first=True)
-    for d in range(1, hi + 1):
-        ring_step(1, d)
-        if d <= lo:
+    def grad_step(d):
+        if d == 0:
+            grad_block(z, first=True)
+        elif d <= lo:
 
             def both(i, carry):
                 grad_block(plane_at(d - 2 * d * i))
@@ -655,9 +663,26 @@
             lax.fori_loop(0, 2, both, 0)
         else:
             grad_block(plane_at(d))
-    gsend[...] = gacc[0].astype(BF16)
-    grad_copy().start()
+
+    middle = max(1, hi // 2)
+
+    @pl.when(core == 1)
+    def _():
+        for d in range(middle + 1):
+            if d > 1 or d == hi:
+                ring_step(1, d)
+            grad_step(d)
+
     finish_down(1)
+
+    @pl.when(core == 1)
+    def _():
+        for d in range(middle + 1, hi + 1):
+            ring_step(1, d)
+            grad_step(d)
+        gsend[...] = gacc[0].astype(BF16)
+        grad_copy().start()
+
     state_landing(other, q).wait_recv()
     state_landing(core, 1 - q).wait_recv()
     state_landing(other, 1 - q).wait_recv()

time: 121 us -> 108 us (0.89)
  Pallas kernels: 117 us -> 103 us
    pallas_call x1, Pallas kernels: 117 us -> 103 us  [stack(): pl.pallas_call(functools.partial(stack_kernel, sizes, width), name='stack...]
where the time goes in v2:
time: 108 us; the launch traced here: 107 us
  Pallas kernels  103 us (95%)
  local copies, waits for them, and re-layouts  3.29 us (3%)
    pallas_call x1, Pallas kernels, stack(): pl.pallas_call(functools.partial(stack_kernel, sizes, width), name='stack...  103 us
    unnamed x2, local copies, waits for them, and re-layouts  3.29 us

profile of v2, /device:TPU:1, one launch (start us, length us, event | category | flops | bytes accessed | tf_op | source)
XLA Modules:
  0.0 107.4 jit_solution(3618093677342644512)
XLA Ops:
  0.6 103.4 %stack.1 = (bf16[128,512]{1,0:T(8,128)(2,1)}, bf16[640,256]{1,0:T(8,128)(2,1)}) custom-call(bf16[128,512]{1,0:T(8,128)(2,1)} %tok_ref.1, bf16[1,512]{1,0:T(2,128)(2,1)} %gain_ref.1, bf16[1,256,640]{2,1,0:T(8,128)(2,1)} %up_ref.1, bf16[1,640,256]{2,1,0:T(8,128)(2,1)} %down_ref.1, bf16[1,128,4096]{2,1,0:T(8,128)(2,1)} %cot_ref.1), custom_call_target="tpu_custom_call" | custom-call | tf_op jit(solution)/shard_map/stack/pallas_call | solution.py:738
  104.1 1.6 %copy.9 = bf16[1,128,512]{2,1,0:T(8,128)(2,1)} copy(bf16[1,128,512]{2,1,0:T(8,128)(2,1)} %bitcast.3) | data formatting | bytes 262144
  105.7 1.7 %copy.10 = bf16[1,640,256]{2,1,0:T(8,128)(2,1)} copy(bf16[1,640,256]{2,1,0:T(8,128)(2,1)} %bitcast.2) | data formatting | bytes 655360

commit v3 on v2

--- a/solution.py
+++ b/solution.py
@@ -64,36 +64,22 @@
     gacc,
     gsend,
     grecv,
-    ld,
-    tk_ss,
+    send_sem,
+    load_sem,
     tk_rs,
-    ga_ss,
     ga_rs,
-    z_ss,
     z_rs,
-    f_ss,
     f_rs,
-    c_ss,
     c_rs,
-    cs_ss,
     cs_rs,
-    sq_ss,
     sq_rs,
-    ux_ss,
     ux_rs,
-    ax_ss,
     ax_rs,
-    hd_ss,
     hd_rs,
-    h_ss,
     h_rs,
-    p_ss,
     p_rs,
-    x_ss,
     x_rs,
-    st_ss,
     st_rs,
-    gx_ss,
     gx_rs,
     end_sem,
 ):
@@ -129,28 +115,39 @@
     their_cols = block_of(1 - q, feat)
     my_part = block_of(t, part_rows)
 
+    hops, pushes, others, gain_sends, grad_sends = (send_sem.at[i] for i in range(5))
+
+    def bytes_of(*dims, size=2):
+        count = size
+        for dim in dims:
+            count *= dim
+        return count
+
+    def await_bytes(sem, count):
+        ref = wd.at[pl.ds(0, count // (2 * feat))]
+        pltpu.make_async_copy(ref, ref, sem).wait()
+
+    def down_rows(layer, origin, piece=0, pieces=1):
+        return block_of((layer * nz + origin) * pieces + piece, hidden // pieces)
+
     def tensor_at(off):
         return lax.rem(t + off, nt)
 
     def plane_at(shift):
         return lax.rem(z + nz + shift, nz)
 
-    sends = []
-
     def launch(make, *args, cond=None):
-        make = functools.partial(make, *args)
-        sends.append((make, cond))
         if cond is None:
-            make().start()
+            make(*args).start()
         else:
-            pl.when(cond())(lambda: make().start())
+            pl.when(cond())(lambda: make(*args).start())
 
     loads = [
-        pltpu.make_async_copy(up_ref.at[0], wu.at[core, z], ld.at[0]),
-        pltpu.make_async_copy(tok_ref, tok, ld.at[1]),
-        pltpu.make_async_copy(down_ref.at[0], wd.at[core, z], ld.at[2]),
+        pltpu.make_async_copy(up_ref.at[0], wu.at[core, z], load_sem.at[0]),
+        pltpu.make_async_copy(tok_ref, tok, load_sem.at[0]),
+        pltpu.make_async_copy(down_ref.at[0], wd.at[down_rows(core, z)], load_sem.at[0]),
         pltpu.make_async_copy(
-            cot_ref.at[0, my_part, block_of(z, slice_width)], cb.at[z, my_part], ld.at[3]
+            cot_ref.at[0, my_part, block_of(z, slice_width)], cb.at[z, my_part], load_sem.at[0]
         ),
     ]
     for copy in loads:
@@ -171,17 +168,20 @@
     greet({"section": other, "dp": beside})
 
     gain_f[...] = gain_ref[...].astype(F32)
-    gains[core, t] = gain_f[:, my_cols]
+    gains[core * nt + t] = gain_f[:, my_cols]
     ssq[...] = jnp.zeros_like(ssq)
-    for copy in loads:
-        copy.wait()
+    await_bytes(
+        load_sem.at[0],
+        bytes_of(2, feat, hidden) + bytes_of(rows, slice_width) + bytes_of(part_rows, slice_width),
+    )
     xb[0, t, mine] = tok[core_rows, my_cols]
 
     pl.semaphore_wait(barrier, (nz - 1) + (2 * nt - 1) + nt + 1)
 
-    def weight(layer, kind, origin, piece):
-        buf = wd if kind else wu
-        return buf.at[layer, origin, block_of(piece, buf.shape[2] // PIECES)]
+    def weight(layer, kind, origin, piece, pieces=PIECES):
+        if kind:
+            return wd.at[down_rows(layer, origin, piece, pieces)]
+        return wu.at[layer, origin, block_of(piece, feat // pieces)]
 
     def along(d):
         return plane_at(-sign * d)
@@ -194,7 +194,7 @@
         return remote(
             ref,
             ref,
-            z_ss.at[m, piece, s],
+            hops,
             z_rs.at[m, piece, s],
             {"dp": plane_at(sign) * INNER + q},
         )
@@ -204,7 +204,7 @@
         return remote(
             ref,
             ref,
-            z_ss.at[m, piece, d - 1],
+            hops,
             z_rs.at[m, piece, d - 1],
             {"dp": plane_at(sign) * INNER + q},
         )
@@ -212,20 +212,18 @@
     def push(m, piece, d):
         ref = weight(m // 2, m % 2, along(d), piece)
         return remote(
-            ref, ref, f_ss.at[m, piece, d], f_rs.at[m, piece, d], {"section": other}
-        )
-
-    def pushed(m, piece, d):
-        ref = weight(m // 2, m % 2, against(d), piece)
-        return remote(
-            ref, ref, f_ss.at[m, piece, d], f_rs.at[m, piece, d], {"section": other}
-        )
+            ref, ref, pushes, f_rs.at[m, d], {"section": other}
+        )
+
+    def pushed(m, d):
+        ref = weight(m // 2, m % 2, against(d), 0, 2 if d == hi else 1)
+        return remote(ref, ref, pushes, f_rs.at[m, d], {"section": other})
 
     def push_own(kind, piece):
         ref = weight(core, kind, z, piece)
         m = 2 * core + kind
         return remote(
-            ref, ref, f_ss.at[m, piece, 0], f_rs.at[m, piece, 0], {"section": other}
+            ref, ref, pushes, f_rs.at[m, 0], {"section": other}
         )
 
     def lacks(layer):
@@ -236,11 +234,9 @@
     near_pieces = [other * half + j for j in range(half)]
 
     def begin(m):
-        for piece in range(PIECES):
-
-            @pl.when(core != m // 2)
-            def _():
-                pushed(m, piece, 0).wait_recv()
+        @pl.when(core != m // 2)
+        def _():
+            pushed(m, 0).wait_recv()
 
         for piece in range(PIECES) if lo else far_pieces:
             launch(hop, m, piece, 0)
@@ -268,12 +264,10 @@
         done_rounds[0] = max(done_rounds[0], last)
 
     def take(m, d):
-        for piece in range(PIECES):
-            pushed(m, piece, d).wait_recv()
+        pushed(m, d).wait_recv()
 
     def take_far(m):
-        for piece in near_pieces:
-            pushed(m, piece, hi).wait_recv()
+        pushed(m, hi).wait_recv()
 
     for piece in range(PIECES):
         launch(push_own, 0, piece)
@@ -288,14 +282,10 @@
         return remote(
             tok.at[core_rows, cols],
             xb.at[0, t, mine],
-            tk_ss.at[away, off],
-            tk_rs.at[t, q],
+            others,
+            tk_rs.at[0],
             {"dp": dp, "tensor": tensor_at(off)},
         )
-
-    def token_landing(tensor, cls):
-        ref = xb.at[0, tensor, block_of(cls, h2)]
-        return remote(ref, ref, tk_ss.at[0, 0], tk_rs.at[tensor, cls], {"dp": beside})
 
     for off in far_first(nt) + [0]:
         launch(token_copy, 1, off)
@@ -304,16 +294,16 @@
 
     def gain_copy(away, off):
         return remote(
-            gains.at[core, t],
-            gains.at[core, t],
-            ga_ss.at[away, off],
-            ga_rs.at[core, t],
+            gains.at[core * nt + t],
+            gains.at[core * nt + t],
+            gain_sends,
+            ga_rs.at[0],
             {"section": other if away else core, "tensor": tensor_at(off)},
         )
 
-    def gain_landing(layer, tensor):
-        ref = gains.at[layer, tensor]
-        return remote(ref, ref, ga_ss.at[0, 0], ga_rs.at[layer, tensor], {"section": other})
+    def await_gains(sem):
+        ref = gains.at[pl.ds(0, sections * nt - 1)]
+        pltpu.make_async_copy(ref, ref, sem).wait()
 
     for off in far_first(nt) + [0]:
         launch(gain_copy, 1, off)
@@ -327,38 +317,26 @@
         return remote(
             cot_ref.at[0, my_part, block_of(to, slice_width)],
             cb.at[z, my_part],
-            c_ss.at[m],
-            c_rs.at[z],
+            others,
+            c_rs.at[0],
             {"dp": to * INNER + q},
         )
-
-    def cot_landing(origin):
-        ref = cb.at[origin, my_part]
-        return remote(ref, ref, c_ss.at[0], c_rs.at[origin], {"dp": beside})
 
     @pl.when(core != 0)
     def _():
-        for piece in range(PIECES):
-            pushed(0, piece, 0).wait_recv()
+        pushed(0, 0).wait_recv()
         for piece in range(PIECES) if lo else far_pieces:
             hop(0, piece, 0).start()
 
-    for piece in range(PIECES) if lo else far_pieces:
-        sends.append((functools.partial(hop, 0, piece, 0), None))
     for m in far_first(nz):
         launch(cot_copy, m)
 
     def cot_share(off):
         ref = cb.at[:, my_part]
-        return remote(ref, ref, cs_ss.at[off], cs_rs.at[t], {"tensor": tensor_at(off)})
-
-    def cot_share_landing(tensor):
-        ref = cb.at[:, block_of(tensor, part_rows)]
-        return remote(ref, ref, cs_ss.at[0], cs_rs.at[tensor], {"dp": beside})
+        return remote(ref, ref, others, cs_rs.at[0], {"tensor": tensor_at(off)})
 
     def await_cotangent():
-        for m in range(1, nz):
-            cot_landing(plane_at(m)).wait_recv()
+        await_bytes(c_rs.at[0], bytes_of(nz - 1, part_rows, slice_width))
 
     def share_cotangent(first, last):
         for off in far_first(nt)[first:last]:
@@ -366,7 +344,7 @@
 
     def prepare(layer, block):
         x = xb[layer, block].astype(F32)
-        xg[block] = (x * gains[layer, block]).astype(BF16)
+        xg[block] = (x * gains[layer * nt + block]).astype(BF16)
         square = x * x
         total = ssq[...]
         for lower in range(0, feat, LANES):
@@ -379,7 +357,7 @@
 
     def sum_copy(layer):
         return remote(
-            sq_send.at[layer], sq_recv.at[layer], sq_ss.at[layer], sq_rs.at[layer], {"dp": beside}
+            sq_send.at[layer], sq_recv.at[layer], others, sq_rs.at[layer], {"dp": beside}
         )
 
     def send_sums(layer):
@@ -390,7 +368,7 @@
 
     def up_copy(layer):
         return remote(
-            up_send.at[layer], up_recv.at[layer], ux_ss.at[layer], ux_rs.at[layer], {"dp": beside}
+            up_send.at[layer], up_recv.at[layer], others, ux_rs.at[layer], {"dp": beside}
         )
 
     def send_up(layer):
@@ -399,24 +377,24 @@
 
     def hidden_copy(layer):
         ref = hid.at[layer, mine]
-        return remote(ref, ref, ax_ss.at[layer], ax_rs.at[layer], {"dp": beside})
+        return remote(ref, ref, others, ax_rs.at[layer], {"dp": beside})
 
     def hidden_landing(layer):
         ref = hid.at[layer, theirs]
-        return remote(ref, ref, ax_ss.at[layer], ax_rs.at[layer], {"dp": beside})
+        return remote(ref, ref, others, ax_rs.at[layer], {"dp": beside})
 
     def hidden_give(layer):
         return remote(
             hid.at[layer, mine],
             hg.at[z, core_rows],
-            hd_ss.at[layer],
+            others,
             hd_rs.at[layer],
             {"section": other},
         )
 
     def hidden_given(layer):
         ref = hg.at[z, other_rows]
-        return remote(ref, ref, hd_ss.at[layer], hd_rs.at[layer], {"section": other})
+        return remote(ref, ref, others, hd_rs.at[layer], {"section": other})
 
     def finish_up(layer):
         sum_copy(layer).wait_recv()
@@ -446,7 +424,7 @@
         return remote(
             ref,
             ref,
-            h_ss.at[k, way, s],
+            others,
             h_rs.at[k, way, s],
             {"dp": plane_at(delta) * INNER + q},
         )
@@ -457,7 +435,7 @@
         return remote(
             ref,
             ref,
-            h_ss.at[k, way, d - 1],
+            others,
             h_rs.at[k, way, d - 1],
             {"dp": plane_at(delta) * INNER + q},
         )
@@ -479,20 +457,14 @@
         return remote(
             part_send.at[layer, block],
             part_recv.at[layer, t],
-            p_ss.at[layer, block],
-            p_rs.at[layer, t],
+            others,
+            p_rs.at[layer],
             {"tensor": block},
-        )
-
-    def part_landing(layer, tensor):
-        ref = part_recv.at[layer, tensor]
-        return remote(
-            ref, ref, p_ss.at[layer, tensor], p_rs.at[layer, tensor], {"tensor": tensor}
         )
 
     def down_block(layer, block):
         part_send[layer, block] = jnp.dot(
-            hid[layer], wd[layer, block], preferred_element_type=F32
+            hid[layer], wd[down_rows(layer, block)], preferred_element_type=F32
         ).astype(BF16)
 
         @pl.when(block != t)
@@ -501,33 +473,22 @@
 
     def next_copy(off):
         ref = xb.at[1, t]
-        return remote(ref, ref, x_ss.at[off], x_rs.at[t], {"tensor": tensor_at(off)})
-
-    def next_landing(tensor):
-        ref = xb.at[1, tensor]
-        return remote(ref, ref, x_ss.at[0], x_rs.at[tensor], {"tensor": tensor})
+        return remote(ref, ref, others, x_rs.at[0], {"tensor": tensor_at(off)})
 
     def state_copy(layer, away):
         return remote(
             xb.at[layer + 1, t, theirs if away else mine],
             state_buf.at[core_rows, my_cols],
-            st_ss.at[layer, away],
-            st_rs.at[core, q],
+            others,
+            st_rs.at[0],
             {"section": layer, "dp": beside} if away else {"section": other},
-        )
-
-    def state_landing(from_core, from_class):
-        ref = state_buf.at[block_of(from_core, h2), block_of(from_class, feat)]
-        return remote(
-            ref, ref, st_ss.at[0, 0], st_rs.at[from_core, from_class], {"section": other}
         )
 
     def finish_down(layer):
         value = xb[layer, t].astype(F32) + part_send[layer, t].astype(F32)
+        await_bytes(p_rs.at[layer], bytes_of(nt - 1, rows, feat))
         for off in range(1, nt):
-            tensor = tensor_at(off)
-            part_landing(layer, tensor).wait_recv()
-            value = value + part_recv[layer, tensor].astype(F32)
+            value = value + part_recv[layer, tensor_at(off)].astype(F32)
         xb[layer + 1, t] = value.astype(BF16)
         if layer == 0:
             for off in far_first(nt):
@@ -548,16 +509,11 @@
             gacc[index] = value if first else gacc[index] + value
 
     def grad_copy():
-        return remote(gsend, grecv, gx_ss.at[0], gx_rs.at[0], {"dp": beside})
+        return remote(gsend, grecv, grad_sends, gx_rs.at[0], {"dp": beside})
 
     z_until(0, 2)
-    for off in range(nt):
-        tensor = tensor_at(off)
-        token_landing(tensor, 1 - q).wait_recv()
-        if off:
-            token_landing(tensor, q).wait_recv()
-            gain_landing(core, tensor).wait_recv()
-        gain_landing(other, tensor).wait_recv()
+    await_bytes(tk_rs.at[0], bytes_of(2 * nt - 1, h2, feat))
+    await_gains(ga_rs.at[0])
 
     def prepare_first(block, carry):
         prepare(0, block)
@@ -588,68 +544,75 @@
     finish_up(0)
     share_cotangent(0, nt // 2 - 1)
     z_until(1, hi)
+    ring_step(0, 0)
     down0 = functools.partial(down_block, 0)
     hidden_landing(0).wait_recv()
     down_block(0, z)
     for d in range(1, lo + 1):
         use_near(1, d, down0)
     use_far(1, down0)
-    ring_step(0, 0)
     z_until(2, 1)
     if hi > 1:
         ring_step(0, 1)
     z_until(2, 2)
+    finish_down(0)
+    share_cotangent(nt // 2 - 1, nt)
     if hi > 2:
         ring_step(0, 2)
-    finish_down(0)
-    share_cotangent(nt // 2 - 1, nt)
-    z_until(2, 3)
-    if hi > 3:
-        ring_step(0, 3)
     z_until(2, hi)
-    for d in range(max(1, min(4, hi)), hi + 1):
-        ring_step(0, d)
 
     prepare(1, t)
     for d in range(1, lo + 1):
         take(2, d)
     take_far(2)
     up_block(1, t, first=True)
-    for off in reversed(far_first(nt)):
-        tensor = tensor_at(off)
-        next_landing(tensor).wait_recv()
-        prepare(1, tensor)
-        up_block(1, tensor)
+    z_until(3, 1)
+    await_bytes(x_rs.at[0], bytes_of(nt - 1, rows, feat))
+
+    def up_second(off, carry):
+        prepare(1, tensor_at(off))
+        up_block(1, tensor_at(off))
+        return carry
+
+    lax.fori_loop(1, nt, up_second, 0)
     send_sums(1)
     send_up(1)
-    z_until(3, 1)
-    for off in range(1, nt):
-        cot_share_landing(tensor_at(off)).wait_recv()
-
-    @pl.when(core == 0)
-    def _():
-        grad_block(z, first=True)
-
-        def one(i, carry):
-            grad_block(plane_at(i))
-            return carry
-
-        lax.fori_loop(1, nz, one, 0)
-        gsend[...] = gacc[0].astype(BF16)
-
+    if hi > 3:
+        ring_step(0, 3)
     z_until(3, 2)
     finish_up(1)
-    pl.when(core == 0)(lambda: grad_copy().start())
     ring_step(1, 0)
+    ring_step(0, hi)
+    await_bytes(cs_rs.at[0], bytes_of(nt - 1, nz * part_rows, slice_width))
+
+    def grad_some(first, last):
+        @pl.when(core == 0)
+        def _():
+            if first == 0:
+                grad_block(z, first=True)
+
+            def one(i, carry):
+                grad_block(plane_at(i))
+                return carry
+
+            lax.fori_loop(max(first, 1), last, one, 0)
+
+    z_until(3, 3)
+    grad_some(0, nz // 2)
     z_until(3, hi)
-    if hi > 1:
-        ring_step(1, 1)
+    ring_step(1, 1)
     hidden_landing(1).wait_recv()
     down1 = functools.partial(down_block, 1)
     down_block(1, z)
     for d in range(1, lo + 1):
         use_near(3, d, down1)
     use_far(3, down1)
+    grad_some(nz // 2, nz)
+
+    @pl.when(core == 0)
+    def _():
+        gsend[...] = gacc[0].astype(BF16)
+        grad_copy().start()
 
     def grad_step(d):
         if d == 0:
@@ -669,7 +632,7 @@
     @pl.when(core == 1)
     def _():
         for d in range(middle + 1):
-            if d > 1 or d == hi:
+            if d > 1:
                 ring_step(1, d)
             grad_step(d)
 
@@ -683,9 +646,7 @@
         gsend[...] = gacc[0].astype(BF16)
         grad_copy().start()
 
-    state_landing(other, q).wait_recv()
-    state_landing(core, 1 - q).wait_recv()
-    state_landing(other, 1 - q).wait_recv()
+    await_bytes(st_rs.at[0], bytes_of(3, h2, feat))
     state_store = pltpu.make_async_copy(state_buf, state_out, end_sem.at[0])
     state_store.start()
     grad_copy().wait_recv()
@@ -694,22 +655,21 @@
     grad_store = pltpu.make_async_copy(gsend, grad_out, end_sem.at[1])
     grad_store.start()
 
-    for make, cond in sends:
-        if cond is None:
-            make().wait_send()
-        else:
-            pl.when(cond())(lambda: make().wait_send())
-    for layer in range(sections):
-        for block in range(nt):
-
-            @pl.when(block != t)
-            def _():
-                part_copy(layer, block).wait_send()
-
-    for k in range(2):
-        for way in range(2):
-            for s in range(ring_length(k, way)):
-                ring_copy(k, way, s, core).wait_send()
+    block_bytes = bytes_of(feat, hidden)
+    passed = 2 * sections * (2 * lo + 1) * block_bytes // 2
+    await_bytes(hops, passed)
+    await_bytes(pushes, passed + 2 * block_bytes)
+    await_gains(gain_sends)
+    await_bytes(
+        others,
+        bytes_of(2 * nt - 1, h2, feat)
+        + bytes_of(nz - 1, part_rows, slice_width)
+        + bytes_of(nt - 1, nz * part_rows, slice_width)
+        + sections * bytes_of(h2, LANES, size=4)
+        + (2 * sections + 1 + 2 * (nz - 1)) * bytes_of(h2, hidden)
+        + (sections + 1) * bytes_of(nt - 1, rows, feat)
+        + 3 * bytes_of(h2, feat),
+    )
     state_store.wait()
     grad_store.wait()
 
@@ -732,9 +692,6 @@
     def buf(*dims, dtype=BF16):
         return pltpu.VMEM(dims, dtype)
 
-    def pair(*dims):
-        return [dma(dims)] * 2
-
     return pl.pallas_call(
         functools.partial(stack_kernel, sizes, width),
         name="stack",
@@ -747,9 +704,9 @@
         scratch_shapes=[
             buf(rows, slice_width),
             buf(1, slice_width, dtype=F32),
-            buf(sections, nt, 1, feat, dtype=F32),
+            buf(sections * nt, 1, feat, dtype=F32),
             buf(sections, nz, feat, hidden),
-            buf(sections, nz, hidden, feat),
+            buf(sections * nz * hidden, feat),
             buf(sections + 1, nt, rows, feat),
             buf(nt, rows, feat),
             buf(rows, LANES, dtype=F32),
@@ -767,23 +724,25 @@
             buf(2, hidden, feat, dtype=F32),
             buf(hidden, feat),
             buf(hidden, feat),
-            dma((4,)),
-            dma((2, nt)),
-            dma((nt, INNER)),
-            dma((2, nt)),
-            dma((sections, nt)),
-        ]
-        + pair(2 * sections, PIECES, hi)
-        + pair(2 * sections, PIECES, hi + 1)
-        + pair(nz)
-        + pair(nt)
-        + pair(sections) * 4
-        + pair(2, 2, hi)
-        + pair(sections, nt)
-        + pair(nt)
-        + [dma((sections, 2)), dma((sections, INNER))]
-        + pair(1)
-        + [dma((2,))],
+            dma((5,)),
+            dma((1,)),
+            dma((1,)),
+            dma((1,)),
+            dma((2 * sections, PIECES, hi)),
+            dma((2 * sections, hi + 1)),
+            dma((1,)),
+            dma((1,)),
+            dma((sections,)),
+            dma((sections,)),
+            dma((sections,)),
+            dma((sections,)),
+            dma((2, 2, hi)),
+            dma((sections,)),
+            dma((1,)),
+            dma((1,)),
+            dma((1,)),
+            dma((2,)),
+        ],
         compiler_params=pltpu.CompilerParams(collective_id=0, has_side_effects=True),
     )(tokens, gain, w_up, w_down, cotangent)
 

time: 108 us -> 100 us (0.926)
  Pallas kernels: 103 us -> 96 us
    pallas_call x1, Pallas kernels: 103 us -> 96 us  [stack(): pl.pallas_call(functools.partial(stack_kernel, sizes, width), name='stack...]
where the time goes in v3:
time: 100 us; the launch traced here: 99.9 us
  Pallas kernels  96 us (96%)
  local copies, waits for them, and re-layouts  3.29 us (3%)
    pallas_call x1, Pallas kernels, stack(): pl.pallas_call(functools.partial(stack_kernel, sizes, width), name='stack...  96 us
    unnamed x2, local copies, waits for them, and re-layouts  3.29 us

profile of v3, /device:TPU:1, one launch (start us, length us, event | category | flops | bytes accessed | tf_op | source)
XLA Modules:
  0.0 99.9 jit_solution(3519499917308157781)
XLA Ops:
  0.6 96.0 %stack.1 = (bf16[128,512]{1,0:T(8,128)(2,1)}, bf16[640,256]{1,0:T(8,128)(2,1)}) custom-call(bf16[128,512]{1,0:T(8,128)(2,1)} %tok_ref.1, bf16[1,512]{1,0:T(2,128)(2,1)} %gain_ref.1, bf16[1,256,640]{2,1,0:T(8,128)(2,1)} %up_ref.1, bf16[1,640,256]{2,1,0:T(8,128)(2,1)} %down_ref.1, bf16[1,128,4096]{2,1,0:T(8,128)(2,1)} %cot_ref.1), custom_call_target="tpu_custom_call" | custom-call | tf_op jit(solution)/shard_map/stack/pallas_call | solution.py:695
  96.6 1.6 %copy.9 = bf16[1,128,512]{2,1,0:T(8,128)(2,1)} copy(bf16[1,128,512]{2,1,0:T(8,128)(2,1)} %bitcast.3) | data formatting | bytes 262144
  98.2 1.7 %copy.10 = bf16[1,640,256]{2,1,0:T(8,128)(2,1)} copy(bf16[1,640,256]{2,1,0:T(8,128)(2,1)} %bitcast.2) | data formatting | bytes 655360

commit v4 on v3

--- a/solution.py
+++ b/solution.py
@@ -1,4 +1,5 @@
 import functools
+import itertools
 
 import jax
 import jax.numpy as jnp
@@ -13,8 +14,10 @@
 
 MESH = pl.DeviceIdType.MESH
 LANES = 128
-PIECES = 4
+PIECES = 8
 INNER = 2
+RING_PARTS = 2
+VMEM_BYTES = 40 * 1024 * 1024
 
 
 def far_first(count):
@@ -40,8 +43,9 @@
     up_ref,
     down_ref,
     cot_ref,
-    state_out,
-    grad_out,
+    state_buf,
+    near_out,
+    grecv,
     tok,
     gain_f,
     gains,
@@ -58,12 +62,10 @@
     hid,
     part_send,
     part_recv,
-    state_buf,
     hg,
     cb,
     gacc,
     gsend,
-    grecv,
     send_sem,
     load_sem,
     tk_rs,
@@ -81,7 +83,6 @@
     x_rs,
     st_rs,
     gx_rs,
-    end_sem,
 ):
     sections, dp_count, nt = sizes
     nz = dp_count // INNER
@@ -418,25 +419,29 @@
     def ring_length(k, way):
         return hi if k == way else lo
 
-    def ring_copy(k, way, s, layer):
+    def ring_ref(k, part, origin, layer):
+        whose = layer if k == 0 else 1 - layer
+        return hg.at[origin, block_of(whose * RING_PARTS + part, h2 // RING_PARTS)]
+
+    def ring_copy(k, part, way, s, layer):
         delta = 1 if way == 0 else -1
-        ref = hg.at[plane_at(-delta * s), block_of(layer if k == 0 else 1 - layer, h2)]
+        ref = ring_ref(k, part, plane_at(-delta * s), layer)
         return remote(
             ref,
             ref,
             others,
-            h_rs.at[k, way, s],
+            h_rs.at[k * RING_PARTS + part, way, s],
             {"dp": plane_at(delta) * INNER + q},
         )
 
-    def ring_landing(k, way, d, layer):
+    def ring_landing(k, part, way, d, layer):
         delta = 1 if way == 0 else -1
-        ref = hg.at[plane_at(-delta * d), block_of(layer if k == 0 else 1 - layer, h2)]
+        ref = ring_ref(k, part, plane_at(-delta * d), layer)
         return remote(
             ref,
             ref,
             others,
-            h_rs.at[k, way, d - 1],
+            h_rs.at[k * RING_PARTS + part, way, d - 1],
             {"dp": plane_at(delta) * INNER + q},
         )
 
@@ -446,12 +451,12 @@
             for k in range(2):
                 if d == 0 and k == 1:
                     hidden_given(layer).wait_recv()
-                for way in range(2):
+                for part, way in itertools.product(range(RING_PARTS), range(2)):
                     length = ring_length(k, way)
                     if 0 < d <= length:
-                        ring_landing(k, way, d, layer).wait_recv()
+                        ring_landing(k, part, way, d, layer).wait_recv()
                     if d < length:
-                        ring_copy(k, way, d, layer).start()
+                        ring_copy(k, part, way, d, layer).start()
 
     def part_copy(layer, block):
         return remote(
@@ -506,10 +511,15 @@
             value = lax.dot_general(
                 left, cb[origin, :, cols], (((0,), (0,)), ((), ())), preferred_element_type=F32
             )
-            gacc[index] = value if first else gacc[index] + value
+            total = near_out if index else gacc
+            total[...] = value if first else total[...] + value
 
     def grad_copy():
         return remote(gsend, grecv, grad_sends, gx_rs.at[0], {"dp": beside})
+
+    def give_grad():
+        gsend[...] = gacc[...].astype(BF16)
+        grad_copy().start()
 
     z_until(0, 2)
     await_bytes(tk_rs.at[0], bytes_of(2 * nt - 1, h2, feat))
@@ -597,22 +607,20 @@
 
             lax.fori_loop(max(first, 1), last, one, 0)
 
+    grad_some(0, nz)
+    pl.when(core == 0)(lambda: give_grad())
     z_until(3, 3)
-    grad_some(0, nz // 2)
+    if hi > 1:
+        ring_step(1, 1)
     z_until(3, hi)
-    ring_step(1, 1)
     hidden_landing(1).wait_recv()
     down1 = functools.partial(down_block, 1)
     down_block(1, z)
     for d in range(1, lo + 1):
+        if d == lo and hi > 2:
+            ring_step(1, 2)
         use_near(3, d, down1)
     use_far(3, down1)
-    grad_some(nz // 2, nz)
-
-    @pl.when(core == 0)
-    def _():
-        gsend[...] = gacc[0].astype(BF16)
-        grad_copy().start()
 
     def grad_step(d):
         if d == 0:
@@ -627,33 +635,26 @@
         else:
             grad_block(plane_at(d))
 
-    middle = max(1, hi // 2)
-
-    @pl.when(core == 1)
-    def _():
-        for d in range(middle + 1):
-            if d > 1:
-                ring_step(1, d)
-            grad_step(d)
-
+    ring_done = [2 if hi > 2 else 1 if hi > 1 else 0]
+
+    def ring_and_grad(first, last):
+        @pl.when(core == 1)
+        def _():
+            for d in range(first, last):
+                if d > ring_done[0]:
+                    ring_step(1, d)
+                grad_step(d)
+
+    ring_and_grad(0, hi)
     finish_down(1)
 
-    @pl.when(core == 1)
-    def _():
-        for d in range(middle + 1, hi + 1):
-            ring_step(1, d)
-            grad_step(d)
-        gsend[...] = gacc[0].astype(BF16)
-        grad_copy().start()
+    ring_and_grad(hi, hi + 1)
+
+    pl.when(core == 1)(lambda: give_grad())
 
     await_bytes(st_rs.at[0], bytes_of(3, h2, feat))
-    state_store = pltpu.make_async_copy(state_buf, state_out, end_sem.at[0])
-    state_store.start()
     grad_copy().wait_recv()
     grad_copy().wait_send()
-    gsend[...] = (gacc[1] + grecv[...].astype(F32)).astype(BF16)
-    grad_store = pltpu.make_async_copy(gsend, grad_out, end_sem.at[1])
-    grad_store.start()
 
     block_bytes = bytes_of(feat, hidden)
     passed = 2 * sections * (2 * lo + 1) * block_bytes // 2
@@ -670,8 +671,6 @@
         + (sections + 1) * bytes_of(nt - 1, rows, feat)
         + 3 * bytes_of(h2, feat),
     )
-    state_store.wait()
-    grad_store.wait()
 
 
 def stack(sizes, tokens, gain, w_up, w_down, cotangent):
@@ -697,10 +696,11 @@
         name="stack",
         out_shape=(
             jax.ShapeDtypeStruct((rows, slice_width), BF16),
+            jax.ShapeDtypeStruct((hidden, feat), F32),
             jax.ShapeDtypeStruct((hidden, feat), BF16),
         ),
         in_specs=[hbm, vmem, hbm, hbm, hbm],
-        out_specs=(hbm, hbm),
+        out_specs=(vmem, vmem, vmem),
         scratch_shapes=[
             buf(rows, slice_width),
             buf(1, slice_width, dtype=F32),
@@ -718,11 +718,9 @@
             buf(sections, rows, hidden),
             buf(sections, nt, rows, feat),
             buf(sections, nt, rows, feat),
-            buf(rows, slice_width),
             buf(nz, rows, hidden),
             buf(nz, rows, slice_width),
-            buf(2, hidden, feat, dtype=F32),
-            buf(hidden, feat),
+            buf(hidden, feat, dtype=F32),
             buf(hidden, feat),
             dma((5,)),
             dma((1,)),
@@ -736,21 +734,45 @@
             dma((sections,)),
             dma((sections,)),
             dma((sections,)),
-            dma((2, 2, hi)),
+            dma((2 * RING_PARTS, 2, hi)),
             dma((sections,)),
             dma((1,)),
             dma((1,)),
             dma((1,)),
-            dma((2,)),
         ],
-        compiler_params=pltpu.CompilerParams(collective_id=0, has_side_effects=True),
+        compiler_params=pltpu.CompilerParams(
+            collective_id=0, has_side_effects=True, vmem_limit_bytes=VMEM_BYTES
+        ),
     )(tokens, gain, w_up, w_down, cotangent)
+
+
+def finish_kernel(state_ref, near_ref, far_ref, state_out, grad_out):
+    state_out[0] = state_ref[...]
+    grad_out[0] = (near_ref[...] + far_ref[...].astype(F32)).astype(BF16)
+
+
+def finish(state, near, far):
+    vmem = pl.BlockSpec(memory_space=pltpu.VMEM)
+    return pl.pallas_call(
+        finish_kernel,
+        name="finish",
+        out_shape=(
+            jax.ShapeDtypeStruct((1, *state.shape), BF16),
+            jax.ShapeDtypeStruct((1, *far.shape), BF16),
+        ),
+        in_specs=[vmem] * 3,
+        out_specs=(vmem, vmem),
+        compiler_params=pltpu.CompilerParams(vmem_limit_bytes=VMEM_BYTES // 4),
+    )(state, near, far)
 
 
 def body(tokens, gain, w_up, w_down, cotangent):
     sizes = (lax.axis_size("section"), lax.axis_size("dp"), lax.axis_size("tensor"))
-    state, grad = stack(sizes, tokens, gain, w_up, w_down, cotangent)
-    return (state[None], grad[None])
+    arrays = [
+        pltpu.with_memory_space_constraint(array, pltpu.HBM)
+        for array in (tokens, gain, w_up, w_down, cotangent)
+    ]
+    return finish(*stack(sizes, *arrays))
 
 
 def solution(mesh):

time: 100 us -> 94.8 us (0.948)
  local copies, waits for them, and re-layouts: 3.29 us -> 0 us
  Pallas kernels: 96 us -> 94.1 us
    unnamed x2 -> x0, local copies, waits for them, and re-layouts: 3.29 us -> none
    pallas_call x1, Pallas kernels: 96 us -> 93.2 us  [stack(): pl.pallas_call(functools.partial(stack_kernel, sizes, width), name='stack...]
where the time goes in v4:
time: 94.8 us; the launch traced here: 94.7 us
  Pallas kernels  94.1 us (99%)
    pallas_call x1, Pallas kernels, stack(): pl.pallas_call(functools.partial(stack_kernel, sizes, width), name='stack...  93.2 us

profile of v4, /device:TPU:1, one launch (start us, length us, event | category | flops | bytes accessed | tf_op | source)
XLA Modules:
  0.0 94.7 jit_solution(13284390939931425221)
XLA Ops:
  0.6 93.2 %stack.1 = (bf16[128,512]{1,0:T(8,128)(2,1)S(1)}, f32[640,256]{1,0:T(8,128)S(1)}, bf16[640,256]{1,0:T(8,128)(2,1)S(1)}) custom-call(bf16[128,512]{1,0:T(8,128)(2,1)} %tok_ref.1, bf16[1,512]{1,0:T(2,128)(2,1)} %gain_ref.1, bf16[1,256,640]{2,1,0:T(8,128)(2,1)} %up_ref.1, bf16[1,640,256]{2,1,0:T(8,128)(2,1)} %down_ref.1, bf16[1,128,4096]{2,1,0:T(8,128)(2,1)} %cot_ref.1), custom_call_target="tpu_custom_call" | custom-call | tf_op jit(solution)/shard_map/stack/pallas_call | solution.py:694
  93.9 0.8 finish.1

commit v5 on v4

--- a/solution.py
+++ b/solution.py
@@ -14,7 +14,7 @@
 
 MESH = pl.DeviceIdType.MESH
 LANES = 128
-PIECES = 8
+PIECES = 4
 INNER = 2
 RING_PARTS = 2
 VMEM_BYTES = 40 * 1024 * 1024
@@ -47,6 +47,7 @@
     near_out,
     grecv,
     tok,
+    gain_raw,
     gain_f,
     gains,
     wu,
@@ -151,6 +152,8 @@
             cot_ref.at[0, my_part, block_of(z, slice_width)], cb.at[z, my_part], load_sem.at[0]
         ),
     ]
+    gain_load = pltpu.make_async_copy(gain_ref, gain_raw, load_sem.at[1])
+    gain_load.start()
     for copy in loads:
         copy.start()
 
@@ -168,7 +171,8 @@
             greet({"tensor": tensor_at(off)})
     greet({"section": other, "dp": beside})
 
-    gain_f[...] = gain_ref[...].astype(F32)
+    gain_load.wait()
+    gain_f[...] = gain_raw[...].astype(F32)
     gains[core * nt + t] = gain_f[:, my_cols]
     ssq[...] = jnp.zeros_like(ssq)
     await_bytes(
@@ -196,7 +200,7 @@
             ref,
             ref,
             hops,
-            z_rs.at[m, piece, s],
+            z_rs.at[m % 3, piece, s],
             {"dp": plane_at(sign) * INNER + q},
         )
 
@@ -206,7 +210,7 @@
             ref,
             ref,
             hops,
-            z_rs.at[m, piece, d - 1],
+            z_rs.at[m % 3, piece, d - 1],
             {"dp": plane_at(sign) * INNER + q},
         )
 
@@ -242,27 +246,42 @@
         for piece in range(PIECES) if lo else far_pieces:
             launch(hop, m, piece, 0)
 
-    def advance(m, d):
-        for piece in range(PIECES) if d < lo else far_pieces:
+    def advance(m, d, between=None):
+        far = d >= lo
+        for count, piece in enumerate(far_pieces if far else range(PIECES)):
             landing(m, piece, d).wait_recv()
             if d < hi:
                 launch(hop, m, piece, d)
             launch(push, m, piece, d)
+            if between is not None:
+                between(count)
         if d == max(lo, 1) and m + 1 < 2 * sections:
             begin(m + 1)
         if d == lo:
-            for piece in near_pieces:
+            for count, piece in enumerate(near_pieces):
                 landing(m, piece, d).wait_recv()
                 launch(push, m, piece, d)
+                if between is not None:
+                    between(half + count)
+        elif far and between is not None:
+            for count in range(half, PIECES):
+                between(count)
 
     rounds = [(m, d) for m in range(2 * sections) for d in range(1, hi + 1)]
     done_rounds = [0]
 
-    def z_until(m, d):
+    def z_until(m, d, between=None):
         last = rounds.index((m, min(d, hi))) + 1
         for r in range(done_rounds[0], last):
-            advance(*rounds[r])
+            advance(*rounds[r], between if r == last - 1 else None)
         done_rounds[0] = max(done_rounds[0], last)
+
+    def spread(count, do):
+        def between(step):
+            for i in range(step * count // PIECES, (step + 1) * count // PIECES):
+                do(i)
+
+        return between
 
     def take(m, d):
         pushed(m, d).wait_recv()
@@ -505,9 +524,10 @@
         def _():
             state_buf[core_rows, my_cols] = xb[layer + 1, t, mine]
 
-    def grad_block(origin, first=False):
+    def grad_block(origin, first=False, parts=(0, 1)):
         left = hg[origin]
-        for index, cols in ((0, their_cols), (1, my_cols)):
+        for index in parts:
+            cols = my_cols if index else their_cols
             value = lax.dot_general(
                 left, cb[origin, :, cols], (((0,), (0,)), ((), ())), preferred_element_type=F32
             )
@@ -571,20 +591,16 @@
         ring_step(0, 2)
     z_until(2, hi)
 
-    prepare(1, t)
     for d in range(1, lo + 1):
         take(2, d)
     take_far(2)
-    up_block(1, t, first=True)
-    z_until(3, 1)
     await_bytes(x_rs.at[0], bytes_of(nt - 1, rows, feat))
 
-    def up_second(off, carry):
+    def up_second(off):
         prepare(1, tensor_at(off))
-        up_block(1, tensor_at(off))
-        return carry
-
-    lax.fori_loop(1, nt, up_second, 0)
+        up_block(1, tensor_at(off), first=off == 0)
+
+    z_until(3, 1, spread(nt, up_second))
     send_sums(1)
     send_up(1)
     if hi > 3:
@@ -648,9 +664,14 @@
     ring_and_grad(0, hi)
     finish_down(1)
 
-    ring_and_grad(hi, hi + 1)
-
-    pl.when(core == 1)(lambda: give_grad())
+    @pl.when(core == 1)
+    def _():
+        if hi > ring_done[0]:
+            ring_step(1, hi)
+        grad_block(plane_at(hi), parts=(0,))
+        give_grad()
+        grad_block(plane_at(hi), parts=(1,))
+
 
     await_bytes(st_rs.at[0], bytes_of(3, h2, feat))
     grad_copy().wait_recv()
@@ -699,10 +720,11 @@
             jax.ShapeDtypeStruct((hidden, feat), F32),
             jax.ShapeDtypeStruct((hidden, feat), BF16),
         ),
-        in_specs=[hbm, vmem, hbm, hbm, hbm],
+        in_specs=[hbm] * 5,
         out_specs=(vmem, vmem, vmem),
         scratch_shapes=[
             buf(rows, slice_width),
+            buf(1, slice_width),
             buf(1, slice_width, dtype=F32),
             buf(sections * nt, 1, feat, dtype=F32),
             buf(sections, nz, feat, hidden),
@@ -723,10 +745,10 @@
             buf(hidden, feat, dtype=F32),
             buf(hidden, feat),
             dma((5,)),
+            dma((2,)),
             dma((1,)),
             dma((1,)),
-            dma((1,)),
-            dma((2 * sections, PIECES, hi)),
+            dma((3, PIECES, hi)),
             dma((2 * sections, hi + 1)),
             dma((1,)),
             dma((1,)),

time: 94.8 us -> 93.9 us (level)
  no operation moved by 1% of the time
where the time goes in v5:
time: 93.9 us; the launch traced here: 93.8 us
  Pallas kernels  93.2 us (99%)
    pallas_call x1, Pallas kernels, stack(): pl.pallas_call(functools.partial(stack_kernel, sizes, width), name='stack...  92.4 us

profile of v5, /device:TPU:1, one launch (start us, length us, event | category | flops | bytes accessed | tf_op | source)
XLA Modules:
  0.0 93.8 jit_solution(17889479324977591345)
XLA Ops:
  0.6 92.4 %stack.1 = (bf16[128,512]{1,0:T(8,128)(2,1)S(1)}, f32[640,256]{1,0:T(8,128)S(1)}, bf16[640,256]{1,0:T(8,128)(2,1)S(1)}) custom-call(bf16[128,512]{1,0:T(8,128)(2,1)} %tok_ref.1, bf16[1,512]{1,0:T(2,128)(2,1)} %gain_ref.1, bf16[1,256,640]{2,1,0:T(8,128)(2,1)} %up_ref.1, bf16[1,640,256]{2,1,0:T(8,128)(2,1)} %down_ref.1, bf16[1,128,4096]{2,1,0:T(8,128)(2,1)} %cot_ref.1), custom_call_target="tpu_custom_call" | custom-call | tf_op jit(solution)/shard_map/stack/pallas_call | solution.py:715
  93.0 0.8 finish.1

commit v6 on v5

--- a/solution.py
+++ b/solution.py
@@ -14,7 +14,7 @@
 
 MESH = pl.DeviceIdType.MESH
 LANES = 128
-PIECES = 4
+PIECES = 8
 INNER = 2
 RING_PARTS = 2
 VMEM_BYTES = 40 * 1024 * 1024
@@ -628,15 +628,15 @@
     z_until(3, 3)
     if hi > 1:
         ring_step(1, 1)
-    z_until(3, hi)
     hidden_landing(1).wait_recv()
     down1 = functools.partial(down_block, 1)
     down_block(1, z)
     for d in range(1, lo + 1):
-        if d == lo and hi > 2:
-            ring_step(1, 2)
         use_near(3, d, down1)
+    z_until(3, hi)
     use_far(3, down1)
+    if hi > 2:
+        ring_step(1, 2)
 
     def grad_step(d):
         if d == 0:

time: 93.9 us -> 93.9 us (level)
  no operation moved by 1% of the time
where the time goes in v6:
time: 93.9 us; the launch traced here: 93.8 us
  Pallas kernels  93.2 us (99%)
    pallas_call x1, Pallas kernels, stack(): pl.pallas_call(functools.partial(stack_kernel, sizes, width), name='stack...  92.3 us

profile of v6, /device:TPU:1, one launch (start us, length us, event | category | flops | bytes accessed | tf_op | source)
XLA Modules:
  0.0 93.8 jit_solution(17748318053501533208)
XLA Ops:
  0.6 92.3 %stack.1 = (bf16[128,512]{1,0:T(8,128)(2,1)S(1)}, f32[640,256]{1,0:T(8,128)S(1)}, bf16[640,256]{1,0:T(8,128)(2,1)S(1)}) custom-call(bf16[128,512]{1,0:T(8,128)(2,1)} %tok_ref.1, bf16[1,512]{1,0:T(2,128)(2,1)} %gain_ref.1, bf16[1,256,640]{2,1,0:T(8,128)(2,1)} %up_ref.1, bf16[1,640,256]{2,1,0:T(8,128)(2,1)} %down_ref.1, bf16[1,128,4096]{2,1,0:T(8,128)(2,1)} %cot_ref.1), custom_call_target="tpu_custom_call" | custom-call | tf_op jit(solution)/shard_map/stack/pallas_call | solution.py:715
  93.0 0.8 finish.1

commit v7 on v5

--- a/solution.py
+++ b/solution.py
@@ -342,14 +342,15 @@
             {"dp": to * INNER + q},
         )
 
+    for m in far_first(nz):
+        launch(cot_copy, m)
+
     @pl.when(core != 0)
     def _():
         pushed(0, 0).wait_recv()
         for piece in range(PIECES) if lo else far_pieces:
             hop(0, piece, 0).start()
 
-    for m in far_first(nz):
-        launch(cot_copy, m)
 
     def cot_share(off):
         ref = cb.at[:, my_part]

time: 93.9 us -> 93.9 us (level)
  no operation moved by 1% of the time
where the time goes in v7:
time: 93.9 us; the launch traced here: 93.4 us
  Pallas kernels  92.8 us (99%)
    pallas_call x1, Pallas kernels, stack(): pl.pallas_call(functools.partial(stack_kernel, sizes, width), name='stack...  91.9 us

profile of v7, /device:TPU:1, one launch (start us, length us, event | category | flops | bytes accessed | tf_op | source)
XLA Modules:
  0.0 93.4 jit_solution(885416319560882016)
XLA Ops:
  0.6 91.9 %stack.1 = (bf16[128,512]{1,0:T(8,128)(2,1)S(1)}, f32[640,256]{1,0:T(8,128)S(1)}, bf16[640,256]{1,0:T(8,128)(2,1)S(1)}) custom-call(bf16[128,512]{1,0:T(8,128)(2,1)} %tok_ref.1, bf16[1,512]{1,0:T(2,128)(2,1)} %gain_ref.1, bf16[1,256,640]{2,1,0:T(8,128)(2,1)} %up_ref.1, bf16[1,640,256]{2,1,0:T(8,128)(2,1)} %down_ref.1, bf16[1,128,4096]{2,1,0:T(8,128)(2,1)} %cot_ref.1), custom_call_target="tpu_custom_call" | custom-call | tf_op jit(solution)/shard_map/stack/pallas_call | solution.py:716
  92.6 0.8 finish.1
